TPU v7x, 128 devices: a whole 4x4x4 slice. The times are simulated.
128 devices in a mesh: ep: 8 (over y, core), fs: 16 (over z, x).
Axes of the slice: x: 4, y: 4, z: 4, core: 2. Of those that a mesh axis runs over, the one named last changes fastest.
Arguments:
- grads: bfloat16 [8, 8, 256, 14336], P('ep', None, 'fs'), may hold values from -64 to 64
- counts: int32 [8, 8], replicated, may hold values from 16 to 2047
- weight: bfloat16 [8, 256, 14336], P('ep', 'fs'), may hold values from -3 to 3
- mom: float32 [8, 256, 14336], P('ep', 'fs'), may hold values from -64 to 64
- second: float32 [8, 256, 14336], P('ep', 'fs'), may hold values from 0.1 to 10
- in_weight: float32 [6, 32], replicated, may hold values from -2.5 to 2.5
- in_bias: float32 [32], replicated, may hold values from -3 to 3
- out_weight: float32 [32, 2], replicated, may hold values from -1 to 1
- out_bias: float32 [2], replicated, may hold values from -3 to 3
Outputs:
- new_weight: bfloat16 [8, 256, 14336], P('ep')
- new_mom: float32 [8, 256, 14336], P('ep', 'fs')
- new_second: float32 [8, 256, 14336], P('ep', 'fs')
All inputs are finite; a program needn't handle non-finite values.
Results may differ from a plain program's by a relative error of at most 0.0019.
Values may be sent and summed in bfloat16 or wider, within the bound.
No kernel may reach another device: no remote copies, remote signals or barrier semaphores. Data moves between devices by JAX's collectives and lax.ppermute only.
A program may use at most 64 MiB of HBM per device.

v0:
```python
import jax
import jax.numpy as jnp
import numpy as np
from jax import lax
from jax.experimental import pallas as pl
from jax.experimental.pallas import tpu as pltpu
from jax.sharding import PartitionSpec as P


MOMENTUM_DECAY = 0.9
SECOND_DECAY = 0.99
NORM_EPS = 1e-06
ROOT_EPS = 1e-08
STEP_SCALE = 0.2
EXP_SCALE = 0.5
LANES = 128
CHUNK = 2048
TILE = 1024


SENDS = [[(2, 0)], [(1, 0), (-1, 0)], [(2, 1), (1, 1)], [(-1, 1), (0, 1), (0, 0)]]
EARLY = [(0, 0), (2, 0), (2, 1), (0, 1), (1, 0), (-1, 0)]
LATE = [(1, 1), (-1, 1)]


def peer(ep, dy, dc, cores=2):
    chips = lax.axis_size("ep") // cores
    return (ep // cores + dy) % chips * cores + (ep % cores + dc) % cores


def weighted_sum(scalars, slots, parts, at, start=None):
    ep = lax.axis_index("ep")
    for (dy, dc), part in zip(slots, parts):
        share = scalars[peer(ep, -dy, dc)]
        term = (share * part[:, at].astype(jnp.float32)).astype(jnp.bfloat16).astype(jnp.float32)
        start = term if start is None else start + term
    return start


def early_kernel(scalars, columns_in, mom, second, weight, *refs):
    parts = refs[: len(EARLY)]
    total, mom_here, second_here, weight_here, table, columns, sem = refs[len(EARLY) :]
    pairs = [(mom, mom_here), (second, second_here), (weight, weight_here)]
    copies = [pltpu.make_async_copy(src, dst, sem.at[k]) for k, (src, dst) in enumerate(pairs)]
    for c in copies:
        c.start()
    first = lax.axis_size("ep")
    for h in range(table.shape[0]):
        for j in range(2):
            table[h, j] = jnp.full((8, LANES), scalars[first + 2 * h + j], jnp.float32)
    columns[...] = columns_in[...]

    def chunk(i, carry):
        at = pl.ds(pl.multiple_of(i * CHUNK, CHUNK), CHUNK)
        total[:, at] = weighted_sum(scalars, EARLY, parts, at)
        return carry

    lax.fori_loop(0, total.shape[1] // CHUNK, chunk, 0)
    for c in copies:
        c.wait()


def folded(squares):
    tiles = [
        squares[r : r + 8, k : k + LANES]
        for k in range(0, squares.shape[1], LANES)
        for r in range(0, squares.shape[0], 8)
    ]
    while len(tiles) > 1:
        tiles = [a + b for a, b in zip(tiles[::2], tiles[1::2])] + tiles[len(tiles) // 2 * 2 :]
    return tiles[0]


def moments_kernel(scalars, early, mom, second, *refs):
    parts = refs[: len(LATE)]
    gradient, mom_next, second_next, sums = refs[len(LATE) :]

    def chunk(i, carry):
        at = pl.ds(pl.multiple_of(i * CHUNK, CHUNK), CHUNK)
        grad = weighted_sum(scalars, LATE, parts, at, early[:, at])
        m = MOMENTUM_DECAY * mom[:, at] + (1.0 - MOMENTUM_DECAY) * grad
        gradient[:, at] = grad
        mom_next[:, at] = m
        second_next[:, at] = SECOND_DECAY * second[:, at] + (1.0 - SECOND_DECAY) * grad * grad
        gg, mm = grad * grad, m * m
        return carry[0] + folded(gg), carry[1] + folded(mm)

    zero = jnp.zeros((8, LANES), jnp.float32)
    a, b = lax.fori_loop(0, gradient.shape[1] // CHUNK, chunk, (zero, zero))
    sums[:, :4] = jnp.full((sums.shape[0], 4, LANES), jnp.sum(a), jnp.float32)
    sums[:, 4:] = jnp.full((sums.shape[0], 4, LANES), jnp.sum(b), jnp.float32)


FEATURE_OF = [0, 1, 2, 3] * 4 + [4, 4]
DEPTH = 8 * len(FEATURE_OF) + 16
CONSTANT_ROWS = [(5, 0), (5, 1), (6, 0), (6, 1)]


def first_layer_columns(in_weight, in_bias):
    feature = np.repeat(np.array(FEATURE_OF), 8)
    sublane = np.arange(feature.size) % 8
    feature = np.concatenate([feature, [f for f, _ in CONSTANT_ROWS]])
    seven = jnp.concatenate([in_weight, in_bias[None]])
    picked = jnp.repeat(seven[feature].T, 8, axis=0)
    mask = (np.arange(picked.shape[0])[:, None] % 8 == sublane[None]).astype(np.float32)
    mask = np.concatenate([mask, np.ones((mask.shape[0], len(CONSTANT_ROWS)), np.float32)], axis=1)
    return jnp.pad(picked * mask, ((0, 0), (0, DEPTH - feature.size)))


def update_kernel(row0, entries, sums, table, columns, gradient, mom, second, weight, *refs):
    hid = table.shape[0] - 1
    pre0, pre1 = refs[-2:]
    copies = []
    if row0 == 0:
        out, layer, mom_out, second_out, sem = refs[:5]
        copies = [pltpu.make_async_copy(mom, mom_out, sem.at[0]), pltpu.make_async_copy(second, second_out, sem.at[1])]
    else:
        layer, out = refs[:2]
    for c in copies:
        c.start()
    if row0 == 0:
        norm = jnp.sqrt(jnp.sum(sums[...], axis=0) / entries + NORM_EPS)
        inv = 1.0 / norm
        lane = lax.broadcasted_iota(jnp.int32, (1, DEPTH), 1)
        group = lane // 8
        paired = group < 16
        const0 = 8 * len(FEATURE_OF)
        is_log = (lane == const0) | (lane == const0 + 1)
        scale = jnp.where(paired & (group % 4 == 0), inv[:1, :1], 1.0)
        scale = jnp.where(paired & (group % 4 == 1), inv[4:5, :1], scale)
        scale = jnp.where(is_log, jnp.log(norm[4:5, :1]), scale)
        low = ((group >= 8) & paired) | (group == 17)
        low = low | ((lane >= const0) & (lane % 2 == 1))
        full = columns[...] * scale
        high = full.astype(jnp.bfloat16).astype(jnp.float32)
        layer[...] = jnp.where(low, full - high, high).astype(jnp.bfloat16)

    def split(pair):
        both = jnp.concatenate(pair, axis=0)
        high = both.astype(jnp.bfloat16)
        return high, (both - high.astype(jnp.float32)).astype(jnp.bfloat16)

    def first(i, pre):
        at = pl.ds(pl.multiple_of(i * TILE, TILE), TILE)
        g, m = gradient[row0 : row0 + 8, at], mom[row0 : row0 + 8, at]
        r = lax.rsqrt(second[row0 : row0 + 8, at] + ROOT_EPS)
        w = weight[row0 : row0 + 8, at].astype(jnp.float32)
        high1, low1 = split([g, m])
        high2, low2 = split([m * r, g * r])
        last = jnp.concatenate([w, w], axis=0).astype(jnp.bfloat16)
        ones = jnp.ones((16, TILE), jnp.bfloat16)
        rows = jnp.concatenate([high1, high2, low1, low2, high1, high2, low1, low2, last, ones], axis=0)
        pre[...] = jnp.dot(layer[...], rows, preferred_element_type=jnp.float32)

    def rest(i, pre):
        at = pl.ds(pl.multiple_of(i * TILE, TILE), TILE)
        parts = [slice(k, k + LANES) for k in range(0, TILE, LANES)]
        direction = [table[hid, 0] for _ in parts]
        magnitude = [table[hid, 1] for _ in parts]
        for h in range(hid):
            t0, t1 = table[h, 0], table[h, 1]
            for k, p in enumerate(parts):
                hidden = jnp.maximum(pre[8 * h : 8 * h + 8, p], 0.0)
                direction[k] = direction[k] + t0 * hidden
                magnitude[k] = magnitude[k] + t1 * hidden
        direction = jnp.concatenate(direction, axis=1)
        magnitude = jnp.concatenate(magnitude, axis=1)
        w = weight[row0 : row0 + 8, at].astype(jnp.float32)
        out[:, at] = (w - STEP_SCALE * direction * jnp.exp(EXP_SCALE * magnitude)).astype(jnp.bfloat16)

    tiles = out.shape[1] // TILE
    first(0, pre0)

    def two(i, carry):
        first(2 * i + 1, pre1)
        rest(2 * i, pre0)
        first(2 * i + 2, pre0)
        rest(2 * i + 1, pre1)
        return carry

    lax.fori_loop(0, tiles // 2 - 1, two, 0)
    first(tiles - 1, pre1)
    rest(tiles - 2, pre0)
    rest(tiles - 1, pre1)
    for c in copies:
        c.wait()


def here(value):
    return pltpu.with_memory_space_constraint(value, pltpu.VMEM)


def place_kernel(spots, *refs):
    out, sem = refs[-2], refs[-1]
    at = lax.axis_index("fs")
    z, x = at // 4, at % 4
    copies = []
    for ref, where in zip(refs, spots):
        for p, (half, dz, dx) in enumerate(where):
            row = (((z + dz) % 4) * 4 + (x + dx) % 4) * 2 + half
            src = ref if len(where) == 1 else ref.at[p]
            copies.append(pltpu.make_async_copy(src, out.at[row], sem.at[len(copies)]))
            copies[-1].start()
    for c in copies:
        c.wait()


def place(into, pieces, shape):
    ins = [here(p) for p, _ in pieces]
    specs = [pl.BlockSpec(memory_space=pltpu.VMEM)] * len(ins)
    alias = {}
    if into is not None:
        ins.append(into)
        specs.append(pl.BlockSpec(memory_space=pl.ANY))
        alias = {len(ins) - 1: 0}
    spots = [spot for _, spot in pieces]
    return pl.pallas_call(
        lambda *refs: place_kernel(spots, *refs),
        out_shape=jax.ShapeDtypeStruct(shape, jnp.bfloat16),
        in_specs=specs,
        out_specs=pl.BlockSpec(memory_space=pl.ANY),
        scratch_shapes=[pltpu.SemaphoreType.DMA((sum(map(len, spots)),))],
        compiler_params=pltpu.CompilerParams(vmem_limit_bytes=1 << 20),
        input_output_aliases=alias,
    )(*ins)


def moved(value, dz, dx):
    pairs = []
    for z in range(4):
        for x in range(4):
            pairs.append((z * 4 + x, ((z + dz) % 4) * 4 + (x + dx) % 4))
    return lax.ppermute(value, "fs", pairs)


def update_rows(row0, entries, layer, sums, table, columns, gradient, mom_next, second_next, weight):
    width = gradient.shape[1]
    vmem = pl.BlockSpec(memory_space=pltpu.VMEM)
    arrays = [here(v) for v in (sums, table, columns, gradient, mom_next, second_next, weight)]
    outs, out_specs, sems = [pltpu.VMEM((8, width), jnp.bfloat16)], [vmem], []
    if layer is None:
        outs.append(pltpu.VMEM(columns.shape, jnp.bfloat16))
        outs += [jax.ShapeDtypeStruct(v.shape, v.dtype) for v in (mom_next, second_next)]
        out_specs += [vmem] + [pl.BlockSpec(memory_space=pl.ANY)] * 2
        sems = [pltpu.SemaphoreType.DMA((2,))]
    else:
        arrays.append(here(layer))
    return pl.pallas_call(
        lambda *refs: update_kernel(row0, entries, *refs),
        out_shape=tuple(outs),
        in_specs=[vmem] * len(arrays),
        out_specs=tuple(out_specs),
        scratch_shapes=sems + [pltpu.VMEM((columns.shape[0], TILE), jnp.float32)] * 2,
        compiler_params=pltpu.CompilerParams(vmem_limit_bytes=8 << 20),
    )(*arrays)


def per_device(grads, counts, weight, mom, second, in_weight, in_bias, out_weight, out_bias):
    rows, width = mom.shape[1:]
    n_fs = lax.axis_size("fs")
    counts_f = counts.astype(jnp.float32)
    shares = counts_f / jnp.sum(counts_f, axis=0)
    share = lax.dynamic_index_in_dim(shares, lax.axis_index("ep"), 1, keepdims=False)
    n_ep = lax.axis_size("ep")
    came = {}
    ep = lax.axis_index("ep")
    mine = grads[0]
    for slots in SENDS:
        picked = [lax.dynamic_index_in_dim(mine, peer(ep, *slot), 0, keepdims=False) for slot in slots]
        mine, *picked = lax.optimization_barrier((mine, *picked))
        for slot, part in zip(slots, picked):
            pairs = [(i, int(peer(i, *slot))) for i in range(n_ep)]
            came[slot] = part if slot == (0, 0) else lax.ppermute(part, "ep", pairs)
    columns = first_layer_columns(in_weight, in_bias)
    vmem, hbm = pl.BlockSpec(memory_space=pltpu.VMEM), pl.BlockSpec(memory_space=pl.ANY)
    f32 = pltpu.VMEM((rows, width), jnp.float32)
    hid = out_weight.shape[0]
    scalars = jnp.concatenate([share, out_weight.reshape(-1), out_bias])
    small = pl.BlockSpec(memory_space=pltpu.SMEM)
    early, mom_here, second_here, weight_here, table, columns = pl.pallas_call(
        early_kernel,
        out_shape=(
            f32,
            f32,
            f32,
            pltpu.VMEM((rows, width), jnp.bfloat16),
            pltpu.VMEM((hid + 1, 2, 8, LANES), jnp.float32),
            pltpu.VMEM(columns.shape, jnp.float32),
        ),
        in_specs=[small, vmem, hbm, hbm, hbm] + [vmem] * len(EARLY),
        out_specs=(vmem,) * 6,
        scratch_shapes=[pltpu.SemaphoreType.DMA((3,))],
        compiler_params=pltpu.CompilerParams(vmem_limit_bytes=4 << 20),
    )(scalars, columns, mom[0], second[0], weight[0], *[here(came[k]) for k in EARLY])
    gradient, mom_next, second_next, sums = pl.pallas_call(
        moments_kernel,
        out_shape=(f32, f32, f32, pltpu.VMEM((n_fs, 8, LANES), jnp.float32)),
        in_specs=[small] + [vmem] * (3 + len(LATE)),
        out_specs=(vmem,) * 4,
        compiler_params=pltpu.CompilerParams(vmem_limit_bytes=4 << 20),
    )(scalars, *[here(v) for v in (early, mom_here, second_here)], *[here(came[k]) for k in LATE])

    sums = lax.all_to_all(sums, "fs", split_axis=0, concat_axis=0, tiled=True)
    entries = rows * width * n_fs
    args = (entries, sums, table, columns, gradient, mom_next, second_next, weight_here)
    top, layer, mom_next, second_next = update_rows(0, args[0], None, *args[1:])
    (bottom,) = update_rows(8, args[0], layer, *args[1:])

    def go(value, axis, d):
        return moved(value, *(d * a for a in axis))

    halves = ((0, top, (0, 1), (1, 0)), (1, bottom, (1, 0), (0, 1)))
    stages = [[], [], []]
    for half, own, along, across in halves:
        at = lambda i, j: (half, i * along[0] + j * across[0], i * along[1] + j * across[1])
        before = go(own, along, 1)
        after = go(own, along, -1)
        far = go(own, along, 2)
        own_up = go(own, across, 1)
        own_down = go(own, across, -1)
        own_beyond = go(own_down, across, -1)
        three = jnp.stack([before, after, far])
        where = (-1, 1, 2)
        up = go(three, across, 1)
        down = go(three, across, -1)
        beyond_up = go(up[:2], across, 1)
        beyond_down = go(down[2], across, -1)
        spots = lambda j: [at(i, j) for i in where]
        stages[0] += [(own, [at(0, 0)]), (three, spots(0)), (own_up, [at(0, -1)]), (own_down, [at(0, 1)])]
        stages[1] += [(up, spots(-1)), (down, spots(1)), (own_beyond, [at(0, 2)])]
        stages[2] += [(beyond_up, spots(2)[:2]), (beyond_down, spots(2)[2:])]
    shape = (2 * n_fs, 8, width)
    out = None
    for pieces in stages:
        out = place(out, pieces, shape)
    return (out.reshape(1, n_fs * rows, width), mom_next[None], second_next[None])


def solution(mesh):
    in_specs = (
        P("ep", None, "fs", None),
        P(),
        P("ep", "fs", None),
        P("ep", "fs", None),
        P("ep", "fs", None),
        P(),
        P(),
        P(),
        P(),
    )
    out_specs = (P("ep", None, None), P("ep", "fs", None), P("ep", "fs", None))
    return jax.shard_map(per_device, mesh=mesh, in_specs=in_specs, out_specs=out_specs, check_vma=False)
```

profile of v0, /device:TPU:0, one launch (start us, length us, event | category | flops | bytes accessed | tf_op | source)
XLA Modules:
  0.0 148.5 jit_solution(17484707282424545257)
XLA Ops:
  0.8 1.8 %dynamic-slice_bitcast_fusion.7 = bf16[16,14336]{1,0:T(8,128)(2,1)} fusion(bf16[1,8,16,14336]{3,2,1,0:T(8,128)(2,1)} %param.12, s32[]{:T(128)S(6)} %select_n.114), kind=kLoop, calls=%fused_computation.10 | loop fusion | bytes 917508 | tf_op jit(solution)/shard_map/jit(dynamic_index_in_dim)/squeeze | solution.py:269
  2.7 2.2 %dynamic-slice_bitcast_fusion.5 = (bf16[16,14336]{1,0:T(8,128)(2,1)}, bf16[16,14336]{1,0:T(8,128)(2,1)}) fusion(bf16[8,16,14336]{2,1,0:T(8,128)(2,1)} %bitcast.41, s32[]{:T(128)S(6)} %select_n.118, s32[]{:T(128)S(6)} %select_n.116), kind=kLoop, calls=%fused_computation.8 | loop fusion | bytes 1835016 | tf_op jit(solution)/shard_map/jit(dynamic_index_in_dim)/squeeze | solution.py:269
  4.9 2.3 %dynamic-slice_bitcast_fusion.3 = (bf16[16,14336]{1,0:T(8,128)(2,1)}, bf16[16,14336]{1,0:T(8,128)(2,1)}) fusion(bf16[8,16,14336]{2,1,0:T(8,128)(2,1)} %bitcast.42, s32[]{:T(128)S(6)} %select_n.121, s32[]{:T(128)S(6)} %select_n.120), kind=kLoop, calls=%fused_computation.6 | loop fusion | bytes 1835016 | tf_op jit(solution)/shard_map/jit(dynamic_index_in_dim)/squeeze | solution.py:269
  7.2 2.3 %dynamic-slice_bitcast_fusion = (bf16[16,14336]{1,0:T(8,128)(2,1)S(1)}, bf16[16,14336]{1,0:T(8,128)(2,1)}, bf16[16,14336]{1,0:T(8,128)(2,1)}) fusion(bf16[8,16,14336]{2,1,0:T(8,128)(2,1)} %bitcast.43, s32[]{:T(128)S(6)} %select_n.125, s32[]{:T(128)S(6)} %select_n.124, s32[]{:T(128)S(6)} %select_n.122), kind=kLoop, calls=%fused_computation.3 | loop fusion | bytes 2752524 | tf_op jit(solution)/shard_map/jit(dynamic_index_in_dim)/squeeze | solution.py:269
  9.5 3.4 %collective-permute-start.1 = (bf16[16,14336]{1,0:T(8,128)(2,1)}, bf16[16,14336]{1,0:T(8,128)(2,1)}, u32[]{:S(2)}, u32[]{:S(2)}) collective-permute-start(bf16[16,14336]{1,0:T(8,128)(2,1)} %get-tuple-element.33), channel_id=1, source_target_pairs={{0,80},{16,64},{32,112},{48,96},{64,16},{80,0},{96,48},{112,32},{1... | collective-permute-start | bytes 1376264 | tf_op jit(solution)/shard_map/ppermute | solution.py:273
  12.9 0.7 collective-permute-start.3
  13.6 2.6 %collective-permute-start.4 = (bf16[16,14336]{1,0:T(8,128)(2,1)}, bf16[16,14336]{1,0:T(8,128)(2,1)}, u32[]{:S(2)}, u32[]{:S(2)}) collective-permute-start(bf16[16,14336]{1,0:T(8,128)(2,1)} %get-tuple-element.36), channel_id=1, source_target_pairs={{0,96},{16,112},{32,0},{48,16},{64,32},{80,48},{96,64},{112,80},{1... | collective-permute-start | bytes 1376264 | tf_op jit(solution)/shard_map/ppermute | solution.py:273
  16.2 0.6 reshape.18
  16.9 0.6 pad_clamp_fusion
  17.5 0.6 convert_divide_fusion
  18.1 0.9 collective-permute-start.6
  19.0 5.2 %collective-permute-done.1.refs_2_ = bf16[16,14336]{1,0:T(8,128)(2,1)} collective-permute-done((bf16[16,14336]{1,0:T(8,128)(2,1)}, bf16[16,14336]{1,0:T(8,128)(2,1)}, u32[]{:S(2)}, u32[]{:S(2)}) %collective-permute-start.1) | collective-permute-done | bytes 458784 | tf_op jit(solution)/shard_map/ppermute | solution.py:273
  24.2 1.8 %collective-permute-start.5 = (bf16[16,14336]{1,0:T(8,128)(2,1)}, bf16[16,14336]{1,0:T(8,128)(2,1)}, u32[]{:S(2)}, u32[]{:S(2)}) collective-permute-start(bf16[16,14336]{1,0:T(8,128)(2,1)} %get-tuple-element.40), channel_id=1, source_target_pairs={{0,48},{16,32},{32,80},{48,64},{64,112},{80,96},{96,16},{112,0},{1... | collective-permute-start | bytes 1376264 | tf_op jit(solution)/shard_map/ppermute | solution.py:273
  26.0 0.8 gather_fusion
  26.8 0.7 copy.20
  27.5 0.9 dynamic-slice_reduce_fusion
  28.4 0.8 multiply_bitcast_fusion
  29.2 0.7 pad_maximum_fusion.3.scalars
  29.9 4.8 %collective-permute-done.3.refs_4_ = bf16[16,14336]{1,0:T(8,128)(2,1)} collective-permute-done((bf16[16,14336]{1,0:T(8,128)(2,1)}, bf16[16,14336]{1,0:T(8,128)(2,1)}, u32[]{:S(2)}, u32[]{:S(2)}) %collective-permute-start.3) | collective-permute-done | bytes 458784 | tf_op jit(solution)/shard_map/ppermute | solution.py:273
  35.2 9.4 %collective-permute-done.refs_1_ = bf16[16,14336]{1,0:T(8,128)(2,1)} collective-permute-done((bf16[16,14336]{1,0:T(8,128)(2,1)}, bf16[16,14336]{1,0:T(8,128)(2,1)}, u32[]{:S(2)}, u32[]{:S(2)}) %collective-permute-start) | collective-permute-done | bytes 458784 | tf_op jit(solution)/shard_map/ppermute | solution.py:273
  44.6 3.2 %shard_map.139 = (f32[16,14336]{1,0:T(8,128)S(1)}, f32[16,14336]{1,0:T(8,128)S(1)}, f32[16,14336]{1,0:T(8,128)S(1)}, bf16[16,14336]{1,0:T(8,128)(2,1)S(1)}, f32[...) custom-call(f32[74]{0:T(128)S(1)} %pad_maximum_fusion.3.scalars, f32[256,160]{1,0:T(8,128)S(1)} %pad.4.columns_in, ...), custom_call_target="tpu_custom_call" | custom-call | tf_op jit(solution)/shard_map/pallas_call | solution.py:280
  47.8 5.7 %collective-permute-done.6.refs_1_ = bf16[16,14336]{1,0:T(8,128)(2,1)} collective-permute-done((bf16[16,14336]{1,0:T(8,128)(2,1)}, bf16[16,14336]{1,0:T(8,128)(2,1)}, u32[]{:S(2)}, u32[]{:S(2)}) %collective-permute-start.6) | collective-permute-done | bytes 458784 | tf_op jit(solution)/shard_map/ppermute | solution.py:273
  53.7 2.1 %shard_map.140 = (f32[16,14336]{1,0:T(8,128)S(1)}, f32[16,14336]{1,0:T(8,128)S(1)}, f32[16,14336]{1,0:T(8,128)S(1)}, f32[16,8,128]{2,1,0:T(8,128)S(1)}) custom-call(f32[74]{0:T(128)S(1)} %pad_maximum_fusion.3.scalars, f32[16,14336]{1,0:T(8,128)S(1)} %get-tuple-element.37.early, f32[16,14336]{1,0:T(8,128)S(1)} %get-tuple-element.38.mom, ...), custom_call_target="tpu_custom_call" | custom-call | tf_op jit(solution)/shard_map/pallas_call | solution.py:295
  55.8 15.3 %all_to_all.5.refs_0_ = f32[16,8,128]{2,1,0:T(8,128)S(1)} all-to-all(f32[16,8,128]{2,1,0:T(8,128)S(1)} %get-tuple-element.42), channel_id=1, replica_groups=mesh['ep'=8,'fs'=16] {'fs'}, dimensions={0} | all-to-all | bytes 131072 | tf_op jit(solution)/shard_map/all_to_all | solution.py:303
  71.1 4.3 %shard_map.141 = (bf16[8,14336]{1,0:T(8,128)(2,1)S(1)}, bf16[256,160]{1,0:T(8,128)(2,1)S(1)}, f32[16,14336]{1,0:T(8,128)}, f32[16,14336]{1,0:T(8,128)}) custom-call(f32[16,8,128]{2,1,0:T(8,128)S(1)} %all_to_all.5.refs_0_, f32[33,2,8,128]{3,2,1,0:T(8,128)S(1)} %get-tuple-element.43.refs_1_, f32[256,160]{1,0:T(8,128)S(1)} %get-tuple-element.44.refs_2_, ...), custom_call_target="tpu_custom_call" | custom-call | tf_op jit(solution)/shard_map/pallas_call | solution.py:248
  75.5 4.2 %shard_map.142.refs_4_ = bf16[8,14336]{1,0:T(8,128)(2,1)S(1)} custom-call(f32[16,8,128]{2,1,0:T(8,128)S(1)} %all_to_all.5.refs_0_, f32[33,2,8,128]{3,2,1,0:T(8,128)S(1)} %get-tuple-element.43.refs_1_, f32[256,160]{1,0:T(8,128)S(1)} %get-tuple-element.44.refs_2_, f32[16,14336]{1,0:T(8,128)S(1)} %get-tuple-element.45.refs_3_, ...), custom_call_target="tpu_custom_call" | custom-call | tf_op jit(solution)/shard_map/pallas_call | solution.py:248
  79.7 0.6 collective-permute-start.14
  80.3 2.7 %collective-permute-start.15 = (bf16[8,14336]{1,0:T(8,128)(2,1)S(1)}, bf16[8,14336]{1,0:T(8,128)(2,1)S(1)}, u32[]{:S(2)}, u32[]{:S(2)}) collective-permute-start(bf16[8,14336]{1,0:T(8,128)(2,1)S(1)} %shard_map.142.refs_4_), channel_id=1, source_target_pairs={{0,12},{1,13},{2,14},{3,15},{4,0},{5,1},{6,2},{7,3},{8,4},{9,5},{1... | collective-permute-start | bytes 688136 | tf_op jit(solution)/shard_map/ppermute | solution.py:233
  83.0 1.2 collective-permute-start.23
  84.2 0.9 collective-permute-start.26
  85.0 7.2 %collective-permute-done.14 = bf16[8,14336]{1,0:T(8,128)(2,1)S(1)} collective-permute-done((bf16[8,14336]{1,0:T(8,128)(2,1)S(1)}, bf16[8,14336]{1,0:T(8,128)(2,1)S(1)}, u32[]{:S(2)}, u32[]{:S(2)}) %collective-permute-start.14) | collective-permute-done | bytes 229408 | tf_op jit(solution)/shard_map/ppermute | solution.py:233
  92.2 0.6 collective-permute-start.7
  92.8 2.7 %collective-permute-start.8 = (bf16[8,14336]{1,0:T(8,128)(2,1)S(1)}, bf16[8,14336]{1,0:T(8,128)(2,1)S(1)}, u32[]{:S(2)}, u32[]{:S(2)}) collective-permute-start(bf16[8,14336]{1,0:T(8,128)(2,1)S(1)} %get-tuple-element.49.refs_0_), channel_id=1, source_target_pairs={{0,3},{1,0},{2,1},{3,2},{4,7},{5,4},{6,5},{7,6},{8,11},{9,8},{10,9... | collective-permute-start | bytes 688136 | tf_op jit(solution)/shard_map/ppermute | solution.py:233
  95.9 6.3 %collective-permute-done.7 = bf16[8,14336]{1,0:T(8,128)(2,1)S(1)} collective-permute-done((bf16[8,14336]{1,0:T(8,128)(2,1)S(1)}, bf16[8,14336]{1,0:T(8,128)(2,1)S(1)}, u32[]{:S(2)}, u32[]{:S(2)}) %collective-permute-start.7) | collective-permute-done | bytes 229408 | tf_op jit(solution)/shard_map/ppermute | solution.py:233
  102.3 3.5 %collective-permute-start.19 = (bf16[3,8,14336]{2,1,0:T(8,128)(2,1)S(1)}, bf16[3,8,14336]{2,1,0:T(8,128)(2,1)S(1)}, u32[]{:S(2)}, u32[]{:S(2)}) collective-permute-start(bf16[3,8,14336]{2,1,0:T(8,128)(2,1)S(1)} %pad_maximum_fusion.1.refs_5_), channel_id=1, source_target_pairs={{0,3},{1,0},{2,1},{3,2},{4,7},{5,4},{6,5},{7,6},{8,11},{9,8},{10,9... | collective-permute-start | bytes 2064392 | tf_op jit(solution)/shard_map/ppermute | solution.py:233
  106.4 9.8 %collective-permute-done.19.refs_4_ = bf16[3,8,14336]{2,1,0:T(8,128)(2,1)S(1)} collective-permute-done((bf16[3,8,14336]{2,1,0:T(8,128)(2,1)S(1)}, bf16[3,8,14336]{2,1,0:T(8,128)(2,1)S(1)}, u32[]{:S(2)}, u32[]{:S(2)}) %collective-permute-start.19) | collective-permute-done | bytes 688160 | tf_op jit(solution)/shard_map/ppermute | solution.py:233
  116.2 1.3 collective-permute-start.12
  117.6 0.7 collective-permute-start.21
  118.3 1.5 collective-permute-start.25
  120.2 2.9 %collective-permute-start.24 = (bf16[8,14336]{1,0:T(8,128)(2,1)S(1)}, bf16[8,14336]{1,0:T(8,128)(2,1)S(1)}, u32[]{:S(2)}, u32[]{:S(2)}) collective-permute-start(bf16[8,14336]{1,0:T(8,128)(2,1)S(1)} %collective-permute-done.23.refs_7_), channel_id=1, source_target_pairs={{0,3},{1,0},{2,1},{3,2},{4,7},{5,4},{6,5},{7,6},{8,11},{9,8},{10,9... | collective-permute-start | bytes 688136 | tf_op jit(solution)/shard_map/ppermute | solution.py:233
  123.3 8.5 %collective-permute-done.12.refs_1_ = bf16[3,8,14336]{2,1,0:T(8,128)(2,1)S(1)} collective-permute-done((bf16[3,8,14336]{2,1,0:T(8,128)(2,1)S(1)}, bf16[3,8,14336]{2,1,0:T(8,128)(2,1)S(1)}, u32[]{:S(2)}, u32[]{:S(2)}) %collective-permute-start.12) | collective-permute-done | bytes 688160 | tf_op jit(solution)/shard_map/ppermute | solution.py:233
  131.8 4.9 %collective-permute-done.21.refs_3_ = bf16[8,14336]{1,0:T(8,128)(2,1)S(1)} collective-permute-done((bf16[8,14336]{1,0:T(8,128)(2,1)S(1)}, bf16[8,14336]{1,0:T(8,128)(2,1)S(1)}, u32[]{:S(2)}, u32[]{:S(2)}) %collective-permute-start.21) | collective-permute-done | bytes 229408 | tf_op jit(solution)/shard_map/ppermute | solution.py:233
  136.7 1.3 collective-permute-start.22
  138.1 3.2 %collective-permute-start.20 = (bf16[8,14336]{1,0:T(8,128)(2,1)S(1)}, bf16[8,14336]{1,0:T(8,128)(2,1)S(1)}, u32[]{:S(2)}, u32[]{:S(2)}) collective-permute-start(bf16[8,14336]{1,0:T(8,128)(2,1)S(1)} %slice_bitcast_fusion), channel_id=1, source_target_pairs={{0,3},{1,0},{2,1},{3,2},{4,7},{5,4},{6,5},{7,6},{8,11},{9,8},{10,9... | collective-permute-start | bytes 688136 | tf_op jit(solution)/shard_map/ppermute | solution.py:233
  141.3 1.6 %shard_map.143.refs_6_ = bf16[32,8,14336]{2,1,0:T(8,128)(2,1)} custom-call(bf16[8,14336]{1,0:T(8,128)(2,1)S(1)} %get-tuple-element.49.refs_0_, bf16[3,8,14336]{2,1,0:T(8,128)(2,1)S(1)} %pad_maximum_fusion.refs_1_, bf16[8,14336]{1,0:T(8,128)(2,1)S(1)} %collective-permute-done.25.refs_2_, bf16[8,14336]{1,0:T(8,128)(2,1)S(1)} %collective-permute-done.21.refs_3_, ...), custom_call_target="tpu_custom_call" | custom-call | tf_op jit(solution)/shard_map/pallas_call | solution.py:217
  143.0 1.8 %shard_map.144.refs_4_ = bf16[32,8,14336]{2,1,0:T(8,128)(2,1)} custom-call(bf16[3,8,14336]{2,1,0:T(8,128)(2,1)S(1)} %collective-permute-done.10.refs_0_, bf16[3,8,14336]{2,1,0:T(8,128)(2,1)S(1)} %collective-permute-done.12.refs_1_, bf16[8,14336]{1,0:T(8,128)(2,1)S(1)} %collective-permute-done.22.refs_2_, ...), custom_call_target="tpu_custom_call", output_to_operand_aliasing={{}: (6, {})} | custom-call | tf_op jit(solution)/shard_map/pallas_call | solution.py:217
  144.9 2.5 %collective-permute-done.13.refs_1_ = bf16[8,14336]{1,0:T(8,128)(2,1)S(1)} collective-permute-done((bf16[8,14336]{1,0:T(8,128)(2,1)S(1)}, bf16[8,14336]{1,0:T(8,128)(2,1)S(1)}, u32[]{:S(2)}, u32[]{:S(2)}) %collective-permute-start.13) | collective-permute-done | bytes 229408 | tf_op jit(solution)/shard_map/ppermute | solution.py:233
  147.3 1.1 shard_map.145
  (54 shorter events, 2.6 us)
Async XLA Ops:
  0.8 15.4 %copy-start.6 = (f32[32,2]{0,1:T(2,128)S(1)}, f32[32,2]{0,1:T(2,128)}, u32[]{:S(2)}) copy-start(f32[32,2]{0,1:T(2,128)} %param.19) | copy-start | bytes 772
  0.8 16.1 %copy-start.7 = (s32[148]{0:T(256)S(1)}, s32[148]{0:T(256)}, u32[]{:S(2)}) copy-start(s32[148]{0:T(256)} %constant.157) | copy-start | bytes 1780
  0.8 16.7 %copy-start.4 = (s32[8,8]{1,0:T(8,128)S(1)}, s32[8,8]{1,0:T(8,128)}, u32[]{:S(2)}) copy-start(s32[8,8]{1,0:T(8,128)} %param.13) | copy-start | bytes 772
  0.8 25.2 %copy-start.5 = (f32[6,32]{1,0:T(8,128)S(1)}, f32[6,32]{1,0:T(8,128)}, u32[]{:S(2)}) copy-start(f32[6,32]{1,0:T(8,128)} %param.17) | copy-start | bytes 2308
  0.8 25.2 %copy-start.8 = (f32[32]{0:T(128)S(1)}, f32[32]{0:T(128)}, u32[]{:S(2)}) copy-start(f32[32]{0:T(128)} %param.18) | copy-start | bytes 388
  2.7 25.7 %copy-start.3 = (f32[32,8,148]{2,1,0:T(8,128)S(1)}, f32[32,8,148]{2,1,0:T(8,128)}, u32[]{:S(2)}) copy-start(f32[32,8,148]{2,1,0:T(8,128)} %constant.156) | copy-start | bytes 454660
  4.9 39.7 %copy-start = (f32[1,16,14336]{2,1,0:T(8,128)S(1)}, f32[1,16,14336]{2,1,0:T(8,128)}, u32[]{:S(2)}) copy-start(f32[1,16,14336]{2,1,0:T(8,128)} %param.15) | copy-start | bytes 2752516
  4.9 39.7 %copy-start.1 = (f32[1,16,14336]{2,1,0:T(8,128)S(1)}, f32[1,16,14336]{2,1,0:T(8,128)}, u32[]{:S(2)}) copy-start(f32[1,16,14336]{2,1,0:T(8,128)} %param.16) | copy-start | bytes 2752516
  4.9 39.7 %copy-start.2 = (bf16[1,16,14336]{2,1,0:T(8,128)(2,1)S(1)}, bf16[1,16,14336]{2,1,0:T(8,128)(2,1)}, u32[]{:S(2)}) copy-start(bf16[1,16,14336]{2,1,0:T(8,128)(2,1)} %param.14) | copy-start | bytes 1376260
  9.5 8.6 %collective-permute-start.2 = (bf16[16,14336]{1,0:T(8,128)(2,1)}, bf16[16,14336]{1,0:T(8,128)(2,1)S(1)}, u32[]{:S(2)}, u32[]{:S(2)}) collective-permute-start(bf16[16,14336]{1,0:T(8,128)(2,1)} %get-tuple-element.34), channel_id=1, source_target_pairs={{0,16},{16,0},{32,48},{48,32},{64,80},{80,64},{96,112},{112,96},{1... | collective-permute-start | bytes 1376264 | tf_op jit(solution)/shard_map/ppermute | solution.py:273
  9.5 14.7 %collective-permute-start.1 = (bf16[16,14336]{1,0:T(8,128)(2,1)}, bf16[16,14336]{1,0:T(8,128)(2,1)}, u32[]{:S(2)}, u32[]{:S(2)}) collective-permute-start(bf16[16,14336]{1,0:T(8,128)(2,1)} %get-tuple-element.33), channel_id=1, source_target_pairs={{0,80},{16,64},{32,112},{48,96},{64,16},{80,0},{96,48},{112,32},{1... | collective-permute-start | bytes 1376264 | tf_op jit(solution)/shard_map/ppermute | solution.py:273
  12.9 21.8 %collective-permute-start.3 = (bf16[16,14336]{1,0:T(8,128)(2,1)}, bf16[16,14336]{1,0:T(8,128)(2,1)}, u32[]{:S(2)}, u32[]{:S(2)}) collective-permute-start(bf16[16,14336]{1,0:T(8,128)(2,1)} %get-tuple-element.35), channel_id=1, source_target_pairs={{0,32},{16,48},{32,64},{48,80},{64,96},{80,112},{96,0},{112,16},{1... | collective-permute-start | bytes 1376264 | tf_op jit(solution)/shard_map/ppermute | solution.py:273
  13.6 21.6 %collective-permute-start.4 = (bf16[16,14336]{1,0:T(8,128)(2,1)}, bf16[16,14336]{1,0:T(8,128)(2,1)}, u32[]{:S(2)}, u32[]{:S(2)}) collective-permute-start(bf16[16,14336]{1,0:T(8,128)(2,1)} %get-tuple-element.36), channel_id=1, source_target_pairs={{0,96},{16,112},{32,0},{48,16},{64,32},{80,48},{96,64},{112,80},{1... | collective-permute-start | bytes 1376264 | tf_op jit(solution)/shard_map/ppermute | solution.py:273
  16.2 28.4 %collective-permute-start = (bf16[16,14336]{1,0:T(8,128)(2,1)}, bf16[16,14336]{1,0:T(8,128)(2,1)}, u32[]{:S(2)}, u32[]{:S(2)}) collective-permute-start(bf16[16,14336]{1,0:T(8,128)(2,1)} %dynamic-slice_bitcast_fusion.7), channel_id=1, source_target_pairs={{0,64},{16,80},{32,96},{48,112},{64,0},{80,16},{96,32},{112,48},{1... | collective-permute-start | bytes 1376264 | tf_op jit(solution)/shard_map/ppermute | solution.py:273
  18.1 35.4 %collective-permute-start.6 = (bf16[16,14336]{1,0:T(8,128)(2,1)}, bf16[16,14336]{1,0:T(8,128)(2,1)}, u32[]{:S(2)}, u32[]{:S(2)}) collective-permute-start(bf16[16,14336]{1,0:T(8,128)(2,1)} %get-tuple-element.41), channel_id=1, source_target_pairs={{0,112},{16,96},{32,16},{48,0},{64,48},{80,32},{96,80},{112,64},{1... | collective-permute-start | bytes 1376264 | tf_op jit(solution)/shard_map/ppermute | solution.py:273
  24.2 29.5 %collective-permute-start.5 = (bf16[16,14336]{1,0:T(8,128)(2,1)}, bf16[16,14336]{1,0:T(8,128)(2,1)}, u32[]{:S(2)}, u32[]{:S(2)}) collective-permute-start(bf16[16,14336]{1,0:T(8,128)(2,1)} %get-tuple-element.40), channel_id=1, source_target_pairs={{0,48},{16,32},{32,80},{48,64},{64,112},{80,96},{96,16},{112,0},{1... | collective-permute-start | bytes 1376264 | tf_op jit(solution)/shard_map/ppermute | solution.py:273
  79.7 12.6 %collective-permute-start.14 = (bf16[8,14336]{1,0:T(8,128)(2,1)S(1)}, bf16[8,14336]{1,0:T(8,128)(2,1)S(1)}, u32[]{:S(2)}, u32[]{:S(2)}) collective-permute-start(bf16[8,14336]{1,0:T(8,128)(2,1)S(1)} %shard_map.142.refs_4_), channel_id=1, source_target_pairs={{0,4},{1,5},{2,6},{3,7},{4,8},{5,9},{6,10},{7,11},{8,12},{9,13},{1... | collective-permute-start | bytes 688136 | tf_op jit(solution)/shard_map/ppermute | solution.py:233
  80.3 12.5 %collective-permute-start.15 = (bf16[8,14336]{1,0:T(8,128)(2,1)S(1)}, bf16[8,14336]{1,0:T(8,128)(2,1)S(1)}, u32[]{:S(2)}, u32[]{:S(2)}) collective-permute-start(bf16[8,14336]{1,0:T(8,128)(2,1)S(1)} %shard_map.142.refs_4_), channel_id=1, source_target_pairs={{0,12},{1,13},{2,14},{3,15},{4,0},{5,1},{6,2},{7,3},{8,4},{9,5},{1... | collective-permute-start | bytes 688136 | tf_op jit(solution)/shard_map/ppermute | solution.py:233
  83.0 12.5 %collective-permute-start.16 = (bf16[8,14336]{1,0:T(8,128)(2,1)S(1)}, bf16[8,14336]{1,0:T(8,128)(2,1)S(1)}, u32[]{:S(2)}, u32[]{:S(2)}) collective-permute-start(bf16[8,14336]{1,0:T(8,128)(2,1)S(1)} %shard_map.142.refs_4_), channel_id=1, source_target_pairs={{0,8},{1,9},{2,10},{3,11},{4,12},{5,13},{6,14},{7,15},{8,0},{9,1},... | collective-permute-start | bytes 688136 | tf_op jit(solution)/shard_map/ppermute | solution.py:233
  83.0 35.3 %collective-permute-start.23 = (bf16[8,14336]{1,0:T(8,128)(2,1)S(1)}, bf16[8,14336]{1,0:T(8,128)(2,1)S(1)}, u32[]{:S(2)}, u32[]{:S(2)}) collective-permute-start(bf16[8,14336]{1,0:T(8,128)(2,1)S(1)} %shard_map.142.refs_4_), channel_id=1, source_target_pairs={{0,3},{1,0},{2,1},{3,2},{4,7},{5,4},{6,5},{7,6},{8,11},{9,8},{10,9... | collective-permute-start | bytes 688136 | tf_op jit(solution)/shard_map/ppermute | solution.py:233
  84.2 39.0 %collective-permute-start.26 = (bf16[8,14336]{1,0:T(8,128)(2,1)S(1)}, bf16[8,14336]{1,0:T(8,128)(2,1)S(1)}, u32[]{:S(2)}, u32[]{:S(2)}) collective-permute-start(bf16[8,14336]{1,0:T(8,128)(2,1)S(1)} %shard_map.142.refs_4_), channel_id=1, source_target_pairs={{0,1},{1,2},{2,3},{3,0},{4,5},{5,6},{6,7},{7,4},{8,9},{9,10},{10,1... | collective-permute-start | bytes 688136 | tf_op jit(solution)/shard_map/ppermute | solution.py:233
  92.2 10.0 %collective-permute-start.7 = (bf16[8,14336]{1,0:T(8,128)(2,1)S(1)}, bf16[8,14336]{1,0:T(8,128)(2,1)S(1)}, u32[]{:S(2)}, u32[]{:S(2)}) collective-permute-start(bf16[8,14336]{1,0:T(8,128)(2,1)S(1)} %get-tuple-element.49.refs_0_), channel_id=1, source_target_pairs={{0,1},{1,2},{2,3},{3,0},{4,5},{5,6},{6,7},{7,4},{8,9},{9,10},{10,1... | collective-permute-start | bytes 688136 | tf_op jit(solution)/shard_map/ppermute | solution.py:233
  92.8 9.4 %collective-permute-start.8 = (bf16[8,14336]{1,0:T(8,128)(2,1)S(1)}, bf16[8,14336]{1,0:T(8,128)(2,1)S(1)}, u32[]{:S(2)}, u32[]{:S(2)}) collective-permute-start(bf16[8,14336]{1,0:T(8,128)(2,1)S(1)} %get-tuple-element.49.refs_0_), channel_id=1, source_target_pairs={{0,3},{1,0},{2,1},{3,2},{4,7},{5,4},{6,5},{7,6},{8,11},{9,8},{10,9... | collective-permute-start | bytes 688136 | tf_op jit(solution)/shard_map/ppermute | solution.py:233
  95.5 10.8 %collective-permute-start.9 = (bf16[8,14336]{1,0:T(8,128)(2,1)S(1)}, bf16[8,14336]{1,0:T(8,128)(2,1)S(1)}, u32[]{:S(2)}, u32[]{:S(2)}) collective-permute-start(bf16[8,14336]{1,0:T(8,128)(2,1)S(1)} %get-tuple-element.49.refs_0_), channel_id=1, source_target_pairs={{0,2},{1,3},{2,0},{3,1},{4,6},{5,7},{6,4},{7,5},{8,10},{9,11},{10,... | collective-permute-start | bytes 688136 | tf_op jit(solution)/shard_map/ppermute | solution.py:233
  102.3 15.3 %collective-permute-start.17 = (bf16[3,8,14336]{2,1,0:T(8,128)(2,1)S(1)}, bf16[3,8,14336]{2,1,0:T(8,128)(2,1)S(1)}, u32[]{:S(2)}, u32[]{:S(2)}) collective-permute-start(bf16[3,8,14336]{2,1,0:T(8,128)(2,1)S(1)} %pad_maximum_fusion.1.refs_5_), channel_id=1, source_target_pairs={{0,1},{1,2},{2,3},{3,0},{4,5},{5,6},{6,7},{7,4},{8,9},{9,10},{10,1... | collective-permute-start | bytes 2064392 | tf_op jit(solution)/shard_map/ppermute | solution.py:233
  102.3 14.0 %collective-permute-start.19 = (bf16[3,8,14336]{2,1,0:T(8,128)(2,1)S(1)}, bf16[3,8,14336]{2,1,0:T(8,128)(2,1)S(1)}, u32[]{:S(2)}, u32[]{:S(2)}) collective-permute-start(bf16[3,8,14336]{2,1,0:T(8,128)(2,1)S(1)} %pad_maximum_fusion.1.refs_5_), channel_id=1, source_target_pairs={{0,3},{1,0},{2,1},{3,2},{4,7},{5,4},{6,5},{7,6},{8,11},{9,8},{10,9... | collective-permute-start | bytes 2064392 | tf_op jit(solution)/shard_map/ppermute | solution.py:233
  106.3 13.9 %collective-permute-start.10 = (bf16[3,8,14336]{2,1,0:T(8,128)(2,1)S(1)}, bf16[3,8,14336]{2,1,0:T(8,128)(2,1)S(1)}, u32[]{:S(2)}, u32[]{:S(2)}) collective-permute-start(bf16[3,8,14336]{2,1,0:T(8,128)(2,1)S(1)} %pad_maximum_fusion.refs_1_), channel_id=1, source_target_pairs={{0,4},{1,5},{2,6},{3,7},{4,8},{5,9},{6,10},{7,11},{8,12},{9,13},{1... | collective-permute-start | bytes 2064392 | tf_op jit(solution)/shard_map/ppermute | solution.py:233
  116.2 15.6 %collective-permute-start.12 = (bf16[3,8,14336]{2,1,0:T(8,128)(2,1)S(1)}, bf16[3,8,14336]{2,1,0:T(8,128)(2,1)S(1)}, u32[]{:S(2)}, u32[]{:S(2)}) collective-permute-start(bf16[3,8,14336]{2,1,0:T(8,128)(2,1)S(1)} %pad_maximum_fusion.refs_1_), channel_id=1, source_target_pairs={{0,12},{1,13},{2,14},{3,15},{4,0},{5,1},{6,2},{7,3},{8,4},{9,5},{1... | collective-permute-start | bytes 2064392 | tf_op jit(solution)/shard_map/ppermute | solution.py:233
  117.6 19.1 %collective-permute-start.21 = (bf16[8,14336]{1,0:T(8,128)(2,1)S(1)}, bf16[8,14336]{1,0:T(8,128)(2,1)S(1)}, u32[]{:S(2)}, u32[]{:S(2)}) collective-permute-start(bf16[8,14336]{1,0:T(8,128)(2,1)S(1)} %get-tuple-element.49.refs_0_), channel_id=1, source_target_pairs={{0,12},{1,13},{2,14},{3,15},{4,0},{5,1},{6,2},{7,3},{8,4},{9,5},{1... | collective-permute-start | bytes 688136 | tf_op jit(solution)/shard_map/ppermute | solution.py:233
  118.3 19.8 %collective-permute-start.25 = (bf16[8,14336]{1,0:T(8,128)(2,1)S(1)}, bf16[8,14336]{1,0:T(8,128)(2,1)S(1)}, u32[]{:S(2)}, u32[]{:S(2)}) collective-permute-start(bf16[8,14336]{1,0:T(8,128)(2,1)S(1)} %get-tuple-element.49.refs_0_), channel_id=1, source_target_pairs={{0,4},{1,5},{2,6},{3,7},{4,8},{5,9},{6,10},{7,11},{8,12},{9,13},{1... | collective-permute-start | bytes 688136 | tf_op jit(solution)/shard_map/ppermute | solution.py:233
  120.2 21.1 %collective-permute-start.24 = (bf16[8,14336]{1,0:T(8,128)(2,1)S(1)}, bf16[8,14336]{1,0:T(8,128)(2,1)S(1)}, u32[]{:S(2)}, u32[]{:S(2)}) collective-permute-start(bf16[8,14336]{1,0:T(8,128)(2,1)S(1)} %collective-permute-done.23.refs_7_), channel_id=1, source_target_pairs={{0,3},{1,0},{2,1},{3,2},{4,7},{5,4},{6,5},{7,6},{8,11},{9,8},{10,9... | collective-permute-start | bytes 688136 | tf_op jit(solution)/shard_map/ppermute | solution.py:233
  123.2 24.1 %collective-permute-start.18 = (bf16[2,8,14336]{2,1,0:T(8,128)(2,1)S(1)}, bf16[2,8,14336]{2,1,0:T(8,128)(2,1)S(1)}, u32[]{:S(2)}, u32[]{:S(2)}) collective-permute-start(bf16[2,8,14336]{2,1,0:T(8,128)(2,1)S(1)} %slice.20), channel_id=1, source_target_pairs={{0,1},{1,2},{2,3},{3,0},{4,5},{5,6},{6,7},{7,4},{8,9},{9,10},{10,1... | collective-permute-start | bytes 1376264 | tf_op jit(solution)/shard_map/ppermute | solution.py:233
  131.8 15.5 %collective-permute-start.11 = (bf16[2,8,14336]{2,1,0:T(8,128)(2,1)S(1)}, bf16[2,8,14336]{2,1,0:T(8,128)(2,1)S(1)}, u32[]{:S(2)}, u32[]{:S(2)}) collective-permute-start(bf16[2,8,14336]{2,1,0:T(8,128)(2,1)S(1)} %slice.18), channel_id=1, source_target_pairs={{0,4},{1,5},{2,6},{3,7},{4,8},{5,9},{6,10},{7,11},{8,12},{9,13},{1... | collective-permute-start | bytes 1376264 | tf_op jit(solution)/shard_map/ppermute | solution.py:233
  136.7 6.2 %collective-permute-start.22 = (bf16[8,14336]{1,0:T(8,128)(2,1)S(1)}, bf16[8,14336]{1,0:T(8,128)(2,1)S(1)}, u32[]{:S(2)}, u32[]{:S(2)}) collective-permute-start(bf16[8,14336]{1,0:T(8,128)(2,1)S(1)} %collective-permute-done.21.refs_3_), channel_id=1, source_target_pairs={{0,12},{1,13},{2,14},{3,15},{4,0},{5,1},{6,2},{7,3},{8,4},{9,5},{1... | collective-permute-start | bytes 688136 | tf_op jit(solution)/shard_map/ppermute | solution.py:233
  138.1 6.8 %collective-permute-start.20 = (bf16[8,14336]{1,0:T(8,128)(2,1)S(1)}, bf16[8,14336]{1,0:T(8,128)(2,1)S(1)}, u32[]{:S(2)}, u32[]{:S(2)}) collective-permute-start(bf16[8,14336]{1,0:T(8,128)(2,1)S(1)} %slice_bitcast_fusion), channel_id=1, source_target_pairs={{0,3},{1,0},{2,1},{3,2},{4,7},{5,4},{6,5},{7,6},{8,11},{9,8},{10,9... | collective-permute-start | bytes 688136 | tf_op jit(solution)/shard_map/ppermute | solution.py:233
  141.3 6.0 %collective-permute-start.13 = (bf16[8,14336]{1,0:T(8,128)(2,1)S(1)}, bf16[8,14336]{1,0:T(8,128)(2,1)S(1)}, u32[]{:S(2)}, u32[]{:S(2)}) collective-permute-start(bf16[8,14336]{1,0:T(8,128)(2,1)S(1)} %slice_bitcast_fusion.1), channel_id=1, source_target_pairs={{0,12},{1,13},{2,14},{3,15},{4,0},{5,1},{6,2},{7,3},{8,4},{9,5},{1... | collective-permute-start | bytes 688136 | tf_op jit(solution)/shard_map/ppermute | solution.py:233
where the time goes:
time: 149 us; the launch traced here: 148 us
  waiting for transfers between devices  66 us (44%)
  starting transfers between devices  33 us (22%)
  Pallas kernels  18.4 us (12%)
  blocking collectives  15.3 us (10%)
  local copies, waits for them, and re-layouts  11.9 us (8%)
  other arithmetic  2.9 us (2%)
    ppermute x20, waiting for transfers between devices, moved(): return lax.ppermute(value, 'fs', pairs)  40.2 us
    ppermute x7, waiting for transfers between devices, per_device(): came[slot] = part if slot == (0, 0) else lax.ppermute(part, 'ep', pairs)  25.8 us
    ppermute x20, starting transfers between devices, moved(): return lax.ppermute(value, 'fs', pairs)  23.6 us
    all_to_all x1, blocking collectives, per_device(): sums = lax.all_to_all(sums, 'fs', split_axis=0, concat_axis=0, tiled=True)  15.3 us
    ppermute x7, starting transfers between devices, per_device(): came[slot] = part if slot == (0, 0) else lax.ppermute(part, 'ep', pairs)  9.36 us
    squeeze x4, local copies, waits for them, and re-layouts, per_device(): lax.dynamic_index_in_dim(mine, peer(ep, *slot), 0, keepdims=False)  8.67 us
    pallas_call x2, Pallas kernels, update_rows(): pl.pallas_call(lambda *refs: update_kernel(row0, entries, *refs), out_sha...  8.52 us
    pallas_call x3, Pallas kernels, place(): pl.pallas_call(lambda *refs: place_kernel(spots, *refs), out_shape=jax.Sh...  4.56 us
  transfers between devices with their start and end apart: 27, of which 15 were waited for; matrix products, arithmetic and copies ran while one was open for 4% of the time, Pallas kernels for 4%

commit v1 on v0

--- a/solution.py
+++ b/solution.py
@@ -14,13 +14,13 @@
 STEP_SCALE = 0.2
 EXP_SCALE = 0.5
 LANES = 128
-CHUNK = 2048
-TILE = 1024
-
-
-SENDS = [[(2, 0)], [(1, 0), (-1, 0)], [(2, 1), (1, 1)], [(-1, 1), (0, 1), (0, 0)]]
-EARLY = [(0, 0), (2, 0), (2, 1), (0, 1), (1, 0), (-1, 0)]
-LATE = [(1, 1), (-1, 1)]
+CHUNK = 3584
+TILE = 1792
+
+
+SENDS = [[(2, 0)], [(1, 0), (-1, 0)], [(1, 1), (-1, 1)], [(2, 1), (0, 1), (0, 0)]]
+EARLY = [(0, 0), (2, 0), (0, 1), (1, 0), (-1, 0), (1, 1)]
+LATE = [(-1, 1), (2, 1)]
 
 
 def peer(ep, dy, dc, cores=2):
@@ -310,7 +310,7 @@
         return moved(value, *(d * a for a in axis))
 
     halves = ((0, top, (0, 1), (1, 0)), (1, bottom, (1, 0), (0, 1)))
-    stages = [[], [], []]
+    stages = [[], [], [], []]
     for half, own, along, across in halves:
         at = lambda i, j: (half, i * along[0] + j * across[0], i * along[1] + j * across[1])
         before = go(own, along, 1)
@@ -328,7 +328,7 @@
         spots = lambda j: [at(i, j) for i in where]
         stages[0] += [(own, [at(0, 0)]), (three, spots(0)), (own_up, [at(0, -1)]), (own_down, [at(0, 1)])]
         stages[1] += [(up, spots(-1)), (down, spots(1)), (own_beyond, [at(0, 2)])]
-        stages[2] += [(beyond_up, spots(2)[:2]), (beyond_down, spots(2)[2:])]
+        stages[2 + half] += [(beyond_up, spots(2)[:2]), (beyond_down, spots(2)[2:])]
     shape = (2 * n_fs, 8, width)
     out = None
     for pieces in stages:

time: 149 us -> 144 us (0.966)
  the two profiles are of different devices: /device:TPU:0 before, /device:TPU:1 now
where the time goes in v1:
time: 144 us; the launch traced here: 141 us
  waiting for transfers between devices  61 us (42%)
  starting transfers between devices  31.3 us (22%)
  Pallas kernels  18.7 us (13%)
  blocking collectives  14 us (10%)
  local copies, waits for them, and re-layouts  11.9 us (8%)
  other arithmetic  2.9 us (2%)
    ppermute x20, waiting for transfers between devices, moved(): return lax.ppermute(value, 'fs', pairs)  34.3 us
    ppermute x7, waiting for transfers between devices, per_device(): came[slot] = part if slot == (0, 0) else lax.ppermute(part, 'ep', pairs)  26.7 us
    ppermute x20, starting transfers between devices, moved(): return lax.ppermute(value, 'fs', pairs)  20.9 us
    all_to_all x1, blocking collectives, per_device(): sums = lax.all_to_all(sums, 'fs', split_axis=0, concat_axis=0, tiled=True)  14 us
    ppermute x7, starting transfers between devices, per_device(): came[slot] = part if slot == (0, 0) else lax.ppermute(part, 'ep', pairs)  10.4 us
    squeeze x4, local copies, waits for them, and re-layouts, per_device(): lax.dynamic_index_in_dim(mine, peer(ep, *slot), 0, keepdims=False)  8.67 us
    pallas_call x2, Pallas kernels, update_rows(): pl.pallas_call(lambda *refs: update_kernel(row0, entries, *refs), out_sha...  8.34 us
    pallas_call x4, Pallas kernels, place(): pl.pallas_call(lambda *refs: place_kernel(spots, *refs), out_shape=jax.Sh...  5.22 us
  transfers between devices with their start and end apart: 27, of which 14 were waited for; matrix products, arithmetic and copies ran while one was open for 4% of the time, Pallas kernels for 8%

profile of v1, /device:TPU:1, one launch (start us, length us, event | category | flops | bytes accessed | tf_op | source)
XLA Modules:
  0.0 141.0 jit_solution(18359285673609965313)
XLA Ops:
  0.8 1.8 %dynamic-slice_bitcast_fusion.7 = bf16[16,14336]{1,0:T(8,128)(2,1)} fusion(bf16[1,8,16,14336]{3,2,1,0:T(8,128)(2,1)} %param.12, s32[]{:T(128)S(6)} %select_n.114), kind=kLoop, calls=%fused_computation.10 | loop fusion | bytes 917508 | tf_op jit(solution)/shard_map/jit(dynamic_index_in_dim)/squeeze | solution.py:269
  2.7 2.2 %dynamic-slice_bitcast_fusion.5 = (bf16[16,14336]{1,0:T(8,128)(2,1)}, bf16[16,14336]{1,0:T(8,128)(2,1)}) fusion(bf16[8,16,14336]{2,1,0:T(8,128)(2,1)} %bitcast.41, s32[]{:T(128)S(6)} %select_n.118, s32[]{:T(128)S(6)} %select_n.116), kind=kLoop, calls=%fused_computation.8 | loop fusion | bytes 1835016 | tf_op jit(solution)/shard_map/jit(dynamic_index_in_dim)/squeeze | solution.py:269
  4.9 2.3 %dynamic-slice_bitcast_fusion.3 = (bf16[16,14336]{1,0:T(8,128)(2,1)}, bf16[16,14336]{1,0:T(8,128)(2,1)}) fusion(bf16[8,16,14336]{2,1,0:T(8,128)(2,1)} %bitcast.42, s32[]{:T(128)S(6)} %select_n.121, s32[]{:T(128)S(6)} %select_n.120), kind=kLoop, calls=%fused_computation.6 | loop fusion | bytes 1835016 | tf_op jit(solution)/shard_map/jit(dynamic_index_in_dim)/squeeze | solution.py:269
  7.2 2.3 %dynamic-slice_bitcast_fusion = (bf16[16,14336]{1,0:T(8,128)(2,1)S(1)}, bf16[16,14336]{1,0:T(8,128)(2,1)}, bf16[16,14336]{1,0:T(8,128)(2,1)}) fusion(bf16[8,16,14336]{2,1,0:T(8,128)(2,1)} %bitcast.43, s32[]{:T(128)S(6)} %select_n.125, s32[]{:T(128)S(6)} %select_n.124, s32[]{:T(128)S(6)} %select_n.122), kind=kLoop, calls=%fused_computation.3 | loop fusion | bytes 2752524 | tf_op jit(solution)/shard_map/jit(dynamic_index_in_dim)/squeeze | solution.py:269
  9.5 1.4 collective-permute-start.1
  10.9 1.3 collective-permute-start.4
  12.2 1.3 collective-permute-start.2
  13.5 1.4 collective-permute-start.3
  14.9 1.4 %collective-permute-start = (bf16[16,14336]{1,0:T(8,128)(2,1)}, bf16[16,14336]{1,0:T(8,128)(2,1)}, u32[]{:S(2)}, u32[]{:S(2)}) collective-permute-start(bf16[16,14336]{1,0:T(8,128)(2,1)} %dynamic-slice_bitcast_fusion.7), channel_id=1, source_target_pairs={{0,64},{16,80},{32,96},{48,112},{64,0},{80,16},{96,32},{112,48},{1... | collective-permute-start | bytes 1376264 | tf_op jit(solution)/shard_map/ppermute | solution.py:273
  16.4 0.6 reshape.18
  18.2 2.8 %collective-permute-start.6 = (bf16[16,14336]{1,0:T(8,128)(2,1)}, bf16[16,14336]{1,0:T(8,128)(2,1)}, u32[]{:S(2)}, u32[]{:S(2)}) collective-permute-start(bf16[16,14336]{1,0:T(8,128)(2,1)} %get-tuple-element.41), channel_id=1, source_target_pairs={{0,80},{16,64},{32,112},{48,96},{64,16},{80,0},{96,48},{112,32},{1... | collective-permute-start | bytes 1376264 | tf_op jit(solution)/shard_map/ppermute | solution.py:273
  21.0 4.2 %collective-permute-done.4.refs_5_ = bf16[16,14336]{1,0:T(8,128)(2,1)} collective-permute-done((bf16[16,14336]{1,0:T(8,128)(2,1)}, bf16[16,14336]{1,0:T(8,128)(2,1)}, u32[]{:S(2)}, u32[]{:S(2)}) %collective-permute-start.4) | collective-permute-done | bytes 458784 | tf_op jit(solution)/shard_map/ppermute | solution.py:273
  25.2 0.8 collective-permute-start.5
  26.1 0.8 gather_fusion
  26.9 0.7 copy.21
  27.6 0.9 dynamic-slice_reduce_fusion
  28.4 0.8 multiply_bitcast_fusion
  29.3 0.7 pad_maximum_fusion.3.scalars
  30.0 4.5 %collective-permute-done.2.refs_3_ = bf16[16,14336]{1,0:T(8,128)(2,1)} collective-permute-done((bf16[16,14336]{1,0:T(8,128)(2,1)}, bf16[16,14336]{1,0:T(8,128)(2,1)}, u32[]{:S(2)}, u32[]{:S(2)}) %collective-permute-start.2) | collective-permute-done | bytes 458784 | tf_op jit(solution)/shard_map/ppermute | solution.py:273
  34.5 10.6 %collective-permute-done.refs_1_ = bf16[16,14336]{1,0:T(8,128)(2,1)} collective-permute-done((bf16[16,14336]{1,0:T(8,128)(2,1)}, bf16[16,14336]{1,0:T(8,128)(2,1)}, u32[]{:S(2)}, u32[]{:S(2)}) %collective-permute-start) | collective-permute-done | bytes 458784 | tf_op jit(solution)/shard_map/ppermute | solution.py:273
  45.2 3.1 %shard_map.139 = (f32[16,14336]{1,0:T(8,128)S(1)}, f32[16,14336]{1,0:T(8,128)S(1)}, f32[16,14336]{1,0:T(8,128)S(1)}, bf16[16,14336]{1,0:T(8,128)(2,1)S(1)}, f32[...) custom-call(f32[74]{0:T(128)S(1)} %pad_maximum_fusion.3.scalars, f32[256,160]{1,0:T(8,128)S(1)} %pad.4.columns_in, ...), custom_call_target="tpu_custom_call" | custom-call | tf_op jit(solution)/shard_map/pallas_call | solution.py:280
  48.3 7.1 %collective-permute-done.6.refs_1_ = bf16[16,14336]{1,0:T(8,128)(2,1)} collective-permute-done((bf16[16,14336]{1,0:T(8,128)(2,1)}, bf16[16,14336]{1,0:T(8,128)(2,1)}, u32[]{:S(2)}, u32[]{:S(2)}) %collective-permute-start.6) | collective-permute-done | bytes 458784 | tf_op jit(solution)/shard_map/ppermute | solution.py:273
  55.6 2.0 %shard_map.140 = (f32[16,14336]{1,0:T(8,128)S(1)}, f32[16,14336]{1,0:T(8,128)S(1)}, f32[16,14336]{1,0:T(8,128)S(1)}, f32[16,8,128]{2,1,0:T(8,128)S(1)}) custom-call(f32[74]{0:T(128)S(1)} %pad_maximum_fusion.3.scalars, f32[16,14336]{1,0:T(8,128)S(1)} %get-tuple-element.37.early, f32[16,14336]{1,0:T(8,128)S(1)} %get-tuple-element.38.mom, ...), custom_call_target="tpu_custom_call" | custom-call | tf_op jit(solution)/shard_map/pallas_call | solution.py:295
  57.6 14.0 %all_to_all.5.refs_0_ = f32[16,8,128]{2,1,0:T(8,128)S(1)} all-to-all(f32[16,8,128]{2,1,0:T(8,128)S(1)} %get-tuple-element.42), channel_id=1, replica_groups=mesh['ep'=8,'fs'=16] {'fs'}, dimensions={0} | all-to-all | bytes 131072 | tf_op jit(solution)/shard_map/all_to_all | solution.py:303
  71.6 4.2 %shard_map.141 = (bf16[8,14336]{1,0:T(8,128)(2,1)S(1)}, bf16[256,160]{1,0:T(8,128)(2,1)S(1)}, f32[16,14336]{1,0:T(8,128)}, f32[16,14336]{1,0:T(8,128)}) custom-call(f32[16,8,128]{2,1,0:T(8,128)S(1)} %all_to_all.5.refs_0_, f32[33,2,8,128]{3,2,1,0:T(8,128)S(1)} %get-tuple-element.43.refs_1_, f32[256,160]{1,0:T(8,128)S(1)} %get-tuple-element.44.refs_2_, ...), custom_call_target="tpu_custom_call" | custom-call | tf_op jit(solution)/shard_map/pallas_call | solution.py:248
  76.4 2.2 %collective-permute-start.15 = (bf16[8,14336]{1,0:T(8,128)(2,1)S(1)}, bf16[8,14336]{1,0:T(8,128)(2,1)S(1)}, u32[]{:S(2)}, u32[]{:S(2)}) collective-permute-start(bf16[8,14336]{1,0:T(8,128)(2,1)S(1)} %get-tuple-element.50.refs_0_), channel_id=1, source_target_pairs={{0,3},{1,0},{2,1},{3,2},{4,7},{5,4},{6,5},{7,6},{8,11},{9,8},{10,9... | collective-permute-start | bytes 688136 | tf_op jit(solution)/shard_map/ppermute | solution.py:233
  78.6 4.1 %shard_map.142.refs_4_ = bf16[8,14336]{1,0:T(8,128)(2,1)S(1)} custom-call(f32[16,8,128]{2,1,0:T(8,128)S(1)} %all_to_all.5.refs_0_, f32[33,2,8,128]{3,2,1,0:T(8,128)S(1)} %get-tuple-element.43.refs_1_, f32[256,160]{1,0:T(8,128)S(1)} %get-tuple-element.44.refs_2_, f32[16,14336]{1,0:T(8,128)S(1)} %get-tuple-element.45.refs_3_, ...), custom_call_target="tpu_custom_call" | custom-call | tf_op jit(solution)/shard_map/pallas_call | solution.py:248
  83.1 2.4 %collective-permute-start.8 = (bf16[8,14336]{1,0:T(8,128)(2,1)S(1)}, bf16[8,14336]{1,0:T(8,128)(2,1)S(1)}, u32[]{:S(2)}, u32[]{:S(2)}) collective-permute-start(bf16[8,14336]{1,0:T(8,128)(2,1)S(1)} %shard_map.142.refs_4_), channel_id=1, source_target_pairs={{0,12},{1,13},{2,14},{3,15},{4,0},{5,1},{6,2},{7,3},{8,4},{9,5},{1... | collective-permute-start | bytes 688136 | tf_op jit(solution)/shard_map/ppermute | solution.py:233
  85.5 1.7 %collective-permute-start.23 = (bf16[8,14336]{1,0:T(8,128)(2,1)S(1)}, bf16[8,14336]{1,0:T(8,128)(2,1)S(1)}, u32[]{:S(2)}, u32[]{:S(2)}) collective-permute-start(bf16[8,14336]{1,0:T(8,128)(2,1)S(1)} %shard_map.142.refs_4_), channel_id=1, source_target_pairs={{0,3},{1,0},{2,1},{3,2},{4,7},{5,4},{6,5},{7,6},{8,11},{9,8},{10,9... | collective-permute-start | bytes 688136 | tf_op jit(solution)/shard_map/ppermute | solution.py:233
  87.8 0.8 collective-permute-start.26
  88.7 0.7 collective-permute-done.7
  89.5 1.0 collective-permute-done.8
  90.8 2.4 %collective-permute-done.9 = bf16[8,14336]{1,0:T(8,128)(2,1)S(1)} collective-permute-done((bf16[8,14336]{1,0:T(8,128)(2,1)S(1)}, bf16[8,14336]{1,0:T(8,128)(2,1)S(1)}, u32[]{:S(2)}, u32[]{:S(2)}) %collective-permute-start.9) | collective-permute-done | bytes 229408 | tf_op jit(solution)/shard_map/ppermute | solution.py:233
  93.3 1.9 %collective-permute-start.19 = (bf16[3,8,14336]{2,1,0:T(8,128)(2,1)S(1)}, bf16[3,8,14336]{2,1,0:T(8,128)(2,1)S(1)}, u32[]{:S(2)}, u32[]{:S(2)}) collective-permute-start(bf16[3,8,14336]{2,1,0:T(8,128)(2,1)S(1)} %pad_maximum_fusion.1.refs_1_), channel_id=1, source_target_pairs={{0,12},{1,13},{2,14},{3,15},{4,0},{5,1},{6,2},{7,3},{8,4},{9,5},{1... | collective-permute-start | bytes 2064392 | tf_op jit(solution)/shard_map/ppermute | solution.py:233
  95.4 10.8 %collective-permute-done.17.refs_0_ = bf16[3,8,14336]{2,1,0:T(8,128)(2,1)S(1)} collective-permute-done((bf16[3,8,14336]{2,1,0:T(8,128)(2,1)S(1)}, bf16[3,8,14336]{2,1,0:T(8,128)(2,1)S(1)}, u32[]{:S(2)}, u32[]{:S(2)}) %collective-permute-start.17) | collective-permute-done | bytes 688160 | tf_op jit(solution)/shard_map/ppermute | solution.py:233
  106.2 7.4 %collective-permute-done.19.refs_1_ = bf16[3,8,14336]{2,1,0:T(8,128)(2,1)S(1)} collective-permute-done((bf16[3,8,14336]{2,1,0:T(8,128)(2,1)S(1)}, bf16[3,8,14336]{2,1,0:T(8,128)(2,1)S(1)}, u32[]{:S(2)}, u32[]{:S(2)}) %collective-permute-start.19) | collective-permute-done | bytes 688160 | tf_op jit(solution)/shard_map/ppermute | solution.py:233
  113.6 1.5 %collective-permute-start.12 = (bf16[3,8,14336]{2,1,0:T(8,128)(2,1)S(1)}, bf16[3,8,14336]{2,1,0:T(8,128)(2,1)S(1)}, u32[]{:S(2)}, u32[]{:S(2)}) collective-permute-start(bf16[3,8,14336]{2,1,0:T(8,128)(2,1)S(1)} %pad_maximum_fusion.refs_5_), channel_id=1, source_target_pairs={{0,3},{1,0},{2,1},{3,2},{4,7},{5,4},{6,5},{7,6},{8,11},{9,8},{10,9... | collective-permute-start | bytes 2064392 | tf_op jit(solution)/shard_map/ppermute | solution.py:233
  115.1 1.3 collective-permute-start.24
  116.4 0.8 collective-permute-done.10.refs_3_
  117.2 2.6 %collective-permute-start.22 = (bf16[8,14336]{1,0:T(8,128)(2,1)S(1)}, bf16[8,14336]{1,0:T(8,128)(2,1)S(1)}, u32[]{:S(2)}, u32[]{:S(2)}) collective-permute-start(bf16[8,14336]{1,0:T(8,128)(2,1)S(1)} %collective-permute-done.21.refs_3_), channel_id=1, source_target_pairs={{0,12},{1,13},{2,14},{3,15},{4,0},{5,1},{6,2},{7,3},{8,4},{9,5},{1... | collective-permute-start | bytes 688136 | tf_op jit(solution)/shard_map/ppermute | solution.py:233
  120.0 2.7 %collective-permute-start.20 = (bf16[8,14336]{1,0:T(8,128)(2,1)S(1)}, bf16[8,14336]{1,0:T(8,128)(2,1)S(1)}, u32[]{:S(2)}, u32[]{:S(2)}) collective-permute-start(bf16[8,14336]{1,0:T(8,128)(2,1)S(1)} %slice_bitcast_fusion), channel_id=1, source_target_pairs={{0,12},{1,13},{2,14},{3,15},{4,0},{5,1},{6,2},{7,3},{8,4},{9,5},{1... | collective-permute-start | bytes 688136 | tf_op jit(solution)/shard_map/ppermute | solution.py:233
  122.6 5.7 %collective-permute-done.12.refs_4_ = bf16[3,8,14336]{2,1,0:T(8,128)(2,1)S(1)} collective-permute-done((bf16[3,8,14336]{2,1,0:T(8,128)(2,1)S(1)}, bf16[3,8,14336]{2,1,0:T(8,128)(2,1)S(1)}, u32[]{:S(2)}, u32[]{:S(2)}) %collective-permute-start.12) | collective-permute-done | bytes 688160 | tf_op jit(solution)/shard_map/ppermute | solution.py:233
  128.4 4.9 %collective-permute-done.24.refs_5_ = bf16[8,14336]{1,0:T(8,128)(2,1)S(1)} collective-permute-done((bf16[8,14336]{1,0:T(8,128)(2,1)S(1)}, bf16[8,14336]{1,0:T(8,128)(2,1)S(1)}, u32[]{:S(2)}, u32[]{:S(2)}) %collective-permute-start.24) | collective-permute-done | bytes 229408 | tf_op jit(solution)/shard_map/ppermute | solution.py:233
  133.3 2.3 %collective-permute-start.13 = (bf16[8,14336]{1,0:T(8,128)(2,1)S(1)}, bf16[8,14336]{1,0:T(8,128)(2,1)S(1)}, u32[]{:S(2)}, u32[]{:S(2)}) collective-permute-start(bf16[8,14336]{1,0:T(8,128)(2,1)S(1)} %slice_bitcast_fusion.1), channel_id=1, source_target_pairs={{0,3},{1,0},{2,1},{3,2},{4,7},{5,4},{6,5},{7,6},{8,11},{9,8},{10,9... | collective-permute-start | bytes 688136 | tf_op jit(solution)/shard_map/ppermute | solution.py:233
  135.5 1.6 %shard_map.143.refs_6_ = bf16[32,8,14336]{2,1,0:T(8,128)(2,1)} custom-call(bf16[8,14336]{1,0:T(8,128)(2,1)S(1)} %get-tuple-element.50.refs_0_, bf16[3,8,14336]{2,1,0:T(8,128)(2,1)S(1)} %pad_maximum_fusion.1.refs_1_, bf16[8,14336]{1,0:T(8,128)(2,1)S(1)} %collective-permute-done.25.refs_2_, bf16[8,14336]{1,0:T(8,128)(2,1)S(1)} %collective-permute-done.21.refs_3_, ...), custom_call_target="tpu_custom_call" | custom-call | tf_op jit(solution)/shard_map/pallas_call | solution.py:217
  137.2 1.8 %shard_map.144.refs_2_ = bf16[32,8,14336]{2,1,0:T(8,128)(2,1)} custom-call(bf16[3,8,14336]{2,1,0:T(8,128)(2,1)S(1)} %collective-permute-done.17.refs_0_, bf16[3,8,14336]{2,1,0:T(8,128)(2,1)S(1)} %collective-permute-done.19.refs_1_, bf16[8,14336]{1,0:T(8,128)(2,1)S(1)} %collective-permute-done.22.refs_2_, ...), custom_call_target="tpu_custom_call", output_to_operand_aliasing={{}: (6, {})} | custom-call | tf_op jit(solution)/shard_map/pallas_call | solution.py:217
  139.0 0.9 shard_map.145.refs_2_
  139.9 0.9 shard_map.146
  (55 shorter events, 4.0 us)
Async XLA Ops:
  0.8 15.5 %copy-start.6 = (f32[32,2]{0,1:T(2,128)S(1)}, f32[32,2]{0,1:T(2,128)}, u32[]{:S(2)}) copy-start(f32[32,2]{0,1:T(2,128)} %param.19) | copy-start | bytes 772
  0.8 16.2 %copy-start.7 = (s32[148]{0:T(256)S(1)}, s32[148]{0:T(256)}, u32[]{:S(2)}) copy-start(s32[148]{0:T(256)} %constant.157) | copy-start | bytes 1780
  0.8 16.8 %copy-start.4 = (s32[8,8]{1,0:T(8,128)S(1)}, s32[8,8]{1,0:T(8,128)}, u32[]{:S(2)}) copy-start(s32[8,8]{1,0:T(8,128)} %param.13) | copy-start | bytes 772
  0.8 25.3 %copy-start.5 = (f32[6,32]{1,0:T(8,128)S(1)}, f32[6,32]{1,0:T(8,128)}, u32[]{:S(2)}) copy-start(f32[6,32]{1,0:T(8,128)} %param.17) | copy-start | bytes 2308
  0.8 25.3 %copy-start.8 = (f32[32]{0:T(128)S(1)}, f32[32]{0:T(128)}, u32[]{:S(2)}) copy-start(f32[32]{0:T(128)} %param.18) | copy-start | bytes 388
  2.7 25.8 %copy-start.3 = (f32[32,8,148]{2,1,0:T(8,128)S(1)}, f32[32,8,148]{2,1,0:T(8,128)}, u32[]{:S(2)}) copy-start(f32[32,8,148]{2,1,0:T(8,128)} %constant.156) | copy-start | bytes 454660
  4.9 40.3 %copy-start = (f32[1,16,14336]{2,1,0:T(8,128)S(1)}, f32[1,16,14336]{2,1,0:T(8,128)}, u32[]{:S(2)}) copy-start(f32[1,16,14336]{2,1,0:T(8,128)} %param.15) | copy-start | bytes 2752516
  4.9 40.3 %copy-start.1 = (f32[1,16,14336]{2,1,0:T(8,128)S(1)}, f32[1,16,14336]{2,1,0:T(8,128)}, u32[]{:S(2)}) copy-start(f32[1,16,14336]{2,1,0:T(8,128)} %param.16) | copy-start | bytes 2752516
  4.9 40.3 %copy-start.2 = (bf16[1,16,14336]{2,1,0:T(8,128)(2,1)S(1)}, bf16[1,16,14336]{2,1,0:T(8,128)(2,1)}, u32[]{:S(2)}) copy-start(bf16[1,16,14336]{2,1,0:T(8,128)(2,1)} %param.14) | copy-start | bytes 1376260
  9.5 8.7 %collective-permute-start.1 = (bf16[16,14336]{1,0:T(8,128)(2,1)}, bf16[16,14336]{1,0:T(8,128)(2,1)S(1)}, u32[]{:S(2)}, u32[]{:S(2)}) collective-permute-start(bf16[16,14336]{1,0:T(8,128)(2,1)} %get-tuple-element.33), channel_id=1, source_target_pairs={{0,16},{16,0},{32,48},{48,32},{64,80},{80,64},{96,112},{112,96},{1... | collective-permute-start | bytes 1376264 | tf_op jit(solution)/shard_map/ppermute | solution.py:273
  10.9 14.3 %collective-permute-start.4 = (bf16[16,14336]{1,0:T(8,128)(2,1)}, bf16[16,14336]{1,0:T(8,128)(2,1)}, u32[]{:S(2)}, u32[]{:S(2)}) collective-permute-start(bf16[16,14336]{1,0:T(8,128)(2,1)} %get-tuple-element.36), channel_id=1, source_target_pairs={{0,48},{16,32},{32,80},{48,64},{64,112},{80,96},{96,16},{112,0},{1... | collective-permute-start | bytes 1376264 | tf_op jit(solution)/shard_map/ppermute | solution.py:273
  12.2 22.4 %collective-permute-start.2 = (bf16[16,14336]{1,0:T(8,128)(2,1)}, bf16[16,14336]{1,0:T(8,128)(2,1)}, u32[]{:S(2)}, u32[]{:S(2)}) collective-permute-start(bf16[16,14336]{1,0:T(8,128)(2,1)} %get-tuple-element.34), channel_id=1, source_target_pairs={{0,32},{16,48},{32,64},{48,80},{64,96},{80,112},{96,0},{112,16},{1... | collective-permute-start | bytes 1376264 | tf_op jit(solution)/shard_map/ppermute | solution.py:273
  13.5 21.1 %collective-permute-start.3 = (bf16[16,14336]{1,0:T(8,128)(2,1)}, bf16[16,14336]{1,0:T(8,128)(2,1)}, u32[]{:S(2)}, u32[]{:S(2)}) collective-permute-start(bf16[16,14336]{1,0:T(8,128)(2,1)} %get-tuple-element.35), channel_id=1, source_target_pairs={{0,96},{16,112},{32,0},{48,16},{64,32},{80,48},{96,64},{112,80},{1... | collective-permute-start | bytes 1376264 | tf_op jit(solution)/shard_map/ppermute | solution.py:273
  14.9 30.3 %collective-permute-start = (bf16[16,14336]{1,0:T(8,128)(2,1)}, bf16[16,14336]{1,0:T(8,128)(2,1)}, u32[]{:S(2)}, u32[]{:S(2)}) collective-permute-start(bf16[16,14336]{1,0:T(8,128)(2,1)} %dynamic-slice_bitcast_fusion.7), channel_id=1, source_target_pairs={{0,64},{16,80},{32,96},{48,112},{64,0},{80,16},{96,32},{112,48},{1... | collective-permute-start | bytes 1376264 | tf_op jit(solution)/shard_map/ppermute | solution.py:273
  18.2 37.2 %collective-permute-start.6 = (bf16[16,14336]{1,0:T(8,128)(2,1)}, bf16[16,14336]{1,0:T(8,128)(2,1)}, u32[]{:S(2)}, u32[]{:S(2)}) collective-permute-start(bf16[16,14336]{1,0:T(8,128)(2,1)} %get-tuple-element.41), channel_id=1, source_target_pairs={{0,80},{16,64},{32,112},{48,96},{64,16},{80,0},{96,48},{112,32},{1... | collective-permute-start | bytes 1376264 | tf_op jit(solution)/shard_map/ppermute | solution.py:273
  25.2 30.3 %collective-permute-start.5 = (bf16[16,14336]{1,0:T(8,128)(2,1)}, bf16[16,14336]{1,0:T(8,128)(2,1)}, u32[]{:S(2)}, u32[]{:S(2)}) collective-permute-start(bf16[16,14336]{1,0:T(8,128)(2,1)} %get-tuple-element.40), channel_id=1, source_target_pairs={{0,112},{16,96},{32,16},{48,0},{64,48},{80,32},{96,80},{112,64},{1... | collective-permute-start | bytes 1376264 | tf_op jit(solution)/shard_map/ppermute | solution.py:273
  75.8 9.6 %collective-permute-start.14 = (bf16[8,14336]{1,0:T(8,128)(2,1)S(1)}, bf16[8,14336]{1,0:T(8,128)(2,1)S(1)}, u32[]{:S(2)}, u32[]{:S(2)}) collective-permute-start(bf16[8,14336]{1,0:T(8,128)(2,1)S(1)} %get-tuple-element.50.refs_0_), channel_id=1, source_target_pairs={{0,1},{1,2},{2,3},{3,0},{4,5},{5,6},{6,7},{7,4},{8,9},{9,10},{10,1... | collective-permute-start | bytes 688136 | tf_op jit(solution)/shard_map/ppermute | solution.py:233
  76.4 9.1 %collective-permute-start.15 = (bf16[8,14336]{1,0:T(8,128)(2,1)S(1)}, bf16[8,14336]{1,0:T(8,128)(2,1)S(1)}, u32[]{:S(2)}, u32[]{:S(2)}) collective-permute-start(bf16[8,14336]{1,0:T(8,128)(2,1)S(1)} %get-tuple-element.50.refs_0_), channel_id=1, source_target_pairs={{0,3},{1,0},{2,1},{3,2},{4,7},{5,4},{6,5},{7,6},{8,11},{9,8},{10,9... | collective-permute-start | bytes 688136 | tf_op jit(solution)/shard_map/ppermute | solution.py:233
  78.6 9.2 %collective-permute-start.16 = (bf16[8,14336]{1,0:T(8,128)(2,1)S(1)}, bf16[8,14336]{1,0:T(8,128)(2,1)S(1)}, u32[]{:S(2)}, u32[]{:S(2)}) collective-permute-start(bf16[8,14336]{1,0:T(8,128)(2,1)S(1)} %get-tuple-element.50.refs_0_), channel_id=1, source_target_pairs={{0,2},{1,3},{2,0},{3,1},{4,6},{5,7},{6,4},{7,5},{8,10},{9,11},{10,... | collective-permute-start | bytes 688136 | tf_op jit(solution)/shard_map/ppermute | solution.py:233
  82.7 6.6 %collective-permute-start.7 = (bf16[8,14336]{1,0:T(8,128)(2,1)S(1)}, bf16[8,14336]{1,0:T(8,128)(2,1)S(1)}, u32[]{:S(2)}, u32[]{:S(2)}) collective-permute-start(bf16[8,14336]{1,0:T(8,128)(2,1)S(1)} %shard_map.142.refs_4_), channel_id=1, source_target_pairs={{0,4},{1,5},{2,6},{3,7},{4,8},{5,9},{6,10},{7,11},{8,12},{9,13},{1... | collective-permute-start | bytes 688136 | tf_op jit(solution)/shard_map/ppermute | solution.py:233
  83.1 7.3 %collective-permute-start.8 = (bf16[8,14336]{1,0:T(8,128)(2,1)S(1)}, bf16[8,14336]{1,0:T(8,128)(2,1)S(1)}, u32[]{:S(2)}, u32[]{:S(2)}) collective-permute-start(bf16[8,14336]{1,0:T(8,128)(2,1)S(1)} %shard_map.142.refs_4_), channel_id=1, source_target_pairs={{0,12},{1,13},{2,14},{3,15},{4,0},{5,1},{6,2},{7,3},{8,4},{9,5},{1... | collective-permute-start | bytes 688136 | tf_op jit(solution)/shard_map/ppermute | solution.py:233
  85.5 7.8 %collective-permute-start.9 = (bf16[8,14336]{1,0:T(8,128)(2,1)S(1)}, bf16[8,14336]{1,0:T(8,128)(2,1)S(1)}, u32[]{:S(2)}, u32[]{:S(2)}) collective-permute-start(bf16[8,14336]{1,0:T(8,128)(2,1)S(1)} %shard_map.142.refs_4_), channel_id=1, source_target_pairs={{0,8},{1,9},{2,10},{3,11},{4,12},{5,13},{6,14},{7,15},{8,0},{9,1},... | collective-permute-start | bytes 688136 | tf_op jit(solution)/shard_map/ppermute | solution.py:233
  85.5 9.8 %collective-permute-start.23 = (bf16[8,14336]{1,0:T(8,128)(2,1)S(1)}, bf16[8,14336]{1,0:T(8,128)(2,1)S(1)}, u32[]{:S(2)}, u32[]{:S(2)}) collective-permute-start(bf16[8,14336]{1,0:T(8,128)(2,1)S(1)} %shard_map.142.refs_4_), channel_id=1, source_target_pairs={{0,3},{1,0},{2,1},{3,2},{4,7},{5,4},{6,5},{7,6},{8,11},{9,8},{10,9... | collective-permute-start | bytes 688136 | tf_op jit(solution)/shard_map/ppermute | solution.py:233
  87.8 32.1 %collective-permute-start.26 = (bf16[8,14336]{1,0:T(8,128)(2,1)S(1)}, bf16[8,14336]{1,0:T(8,128)(2,1)S(1)}, u32[]{:S(2)}, u32[]{:S(2)}) collective-permute-start(bf16[8,14336]{1,0:T(8,128)(2,1)S(1)} %shard_map.142.refs_4_), channel_id=1, source_target_pairs={{0,1},{1,2},{2,3},{3,0},{4,5},{5,6},{6,7},{7,4},{8,9},{9,10},{10,1... | collective-permute-start | bytes 688136 | tf_op jit(solution)/shard_map/ppermute | solution.py:233
  89.4 25.8 %collective-permute-start.21 = (bf16[8,14336]{1,0:T(8,128)(2,1)S(1)}, bf16[8,14336]{1,0:T(8,128)(2,1)S(1)}, u32[]{:S(2)}, u32[]{:S(2)}) collective-permute-start(bf16[8,14336]{1,0:T(8,128)(2,1)S(1)} %get-tuple-element.50.refs_0_), channel_id=1, source_target_pairs={{0,12},{1,13},{2,14},{3,15},{4,0},{5,1},{6,2},{7,3},{8,4},{9,5},{1... | collective-permute-start | bytes 688136 | tf_op jit(solution)/shard_map/ppermute | solution.py:233
  90.4 15.8 %collective-permute-start.17 = (bf16[3,8,14336]{2,1,0:T(8,128)(2,1)S(1)}, bf16[3,8,14336]{2,1,0:T(8,128)(2,1)S(1)}, u32[]{:S(2)}, u32[]{:S(2)}) collective-permute-start(bf16[3,8,14336]{2,1,0:T(8,128)(2,1)S(1)} %pad_maximum_fusion.1.refs_1_), channel_id=1, source_target_pairs={{0,4},{1,5},{2,6},{3,7},{4,8},{5,9},{6,10},{7,11},{8,12},{9,13},{1... | collective-permute-start | bytes 2064392 | tf_op jit(solution)/shard_map/ppermute | solution.py:233
  93.3 20.3 %collective-permute-start.19 = (bf16[3,8,14336]{2,1,0:T(8,128)(2,1)S(1)}, bf16[3,8,14336]{2,1,0:T(8,128)(2,1)S(1)}, u32[]{:S(2)}, u32[]{:S(2)}) collective-permute-start(bf16[3,8,14336]{2,1,0:T(8,128)(2,1)S(1)} %pad_maximum_fusion.1.refs_1_), channel_id=1, source_target_pairs={{0,12},{1,13},{2,14},{3,15},{4,0},{5,1},{6,2},{7,3},{8,4},{9,5},{1... | collective-permute-start | bytes 2064392 | tf_op jit(solution)/shard_map/ppermute | solution.py:233
  95.3 24.7 %collective-permute-start.25 = (bf16[8,14336]{1,0:T(8,128)(2,1)S(1)}, bf16[8,14336]{1,0:T(8,128)(2,1)S(1)}, u32[]{:S(2)}, u32[]{:S(2)}) collective-permute-start(bf16[8,14336]{1,0:T(8,128)(2,1)S(1)} %get-tuple-element.50.refs_0_), channel_id=1, source_target_pairs={{0,4},{1,5},{2,6},{3,7},{4,8},{5,9},{6,10},{7,11},{8,12},{9,13},{1... | collective-permute-start | bytes 688136 | tf_op jit(solution)/shard_map/ppermute | solution.py:233
  106.2 11.0 %collective-permute-start.10 = (bf16[3,8,14336]{2,1,0:T(8,128)(2,1)S(1)}, bf16[3,8,14336]{2,1,0:T(8,128)(2,1)S(1)}, u32[]{:S(2)}, u32[]{:S(2)}) collective-permute-start(bf16[3,8,14336]{2,1,0:T(8,128)(2,1)S(1)} %pad_maximum_fusion.refs_5_), channel_id=1, source_target_pairs={{0,1},{1,2},{2,3},{3,0},{4,5},{5,6},{6,7},{7,4},{8,9},{9,10},{10,1... | collective-permute-start | bytes 2064392 | tf_op jit(solution)/shard_map/ppermute | solution.py:233
  113.6 14.7 %collective-permute-start.12 = (bf16[3,8,14336]{2,1,0:T(8,128)(2,1)S(1)}, bf16[3,8,14336]{2,1,0:T(8,128)(2,1)S(1)}, u32[]{:S(2)}, u32[]{:S(2)}) collective-permute-start(bf16[3,8,14336]{2,1,0:T(8,128)(2,1)S(1)} %pad_maximum_fusion.refs_5_), channel_id=1, source_target_pairs={{0,3},{1,0},{2,1},{3,2},{4,7},{5,4},{6,5},{7,6},{8,11},{9,8},{10,9... | collective-permute-start | bytes 2064392 | tf_op jit(solution)/shard_map/ppermute | solution.py:233
  115.1 18.1 %collective-permute-start.24 = (bf16[8,14336]{1,0:T(8,128)(2,1)S(1)}, bf16[8,14336]{1,0:T(8,128)(2,1)S(1)}, u32[]{:S(2)}, u32[]{:S(2)}) collective-permute-start(bf16[8,14336]{1,0:T(8,128)(2,1)S(1)} %collective-permute-done.23.refs_7_), channel_id=1, source_target_pairs={{0,3},{1,0},{2,1},{3,2},{4,7},{5,4},{6,5},{7,6},{8,11},{9,8},{10,9... | collective-permute-start | bytes 688136 | tf_op jit(solution)/shard_map/ppermute | solution.py:233
  117.2 20.0 %collective-permute-start.22 = (bf16[8,14336]{1,0:T(8,128)(2,1)S(1)}, bf16[8,14336]{1,0:T(8,128)(2,1)S(1)}, u32[]{:S(2)}, u32[]{:S(2)}) collective-permute-start(bf16[8,14336]{1,0:T(8,128)(2,1)S(1)} %collective-permute-done.21.refs_3_), channel_id=1, source_target_pairs={{0,12},{1,13},{2,14},{3,15},{4,0},{5,1},{6,2},{7,3},{8,4},{9,5},{1... | collective-permute-start | bytes 688136 | tf_op jit(solution)/shard_map/ppermute | solution.py:233
  119.9 19.1 %collective-permute-start.18 = (bf16[2,8,14336]{2,1,0:T(8,128)(2,1)S(1)}, bf16[2,8,14336]{2,1,0:T(8,128)(2,1)S(1)}, u32[]{:S(2)}, u32[]{:S(2)}) collective-permute-start(bf16[2,8,14336]{2,1,0:T(8,128)(2,1)S(1)} %slice.20), channel_id=1, source_target_pairs={{0,4},{1,5},{2,6},{3,7},{4,8},{5,9},{6,10},{7,11},{8,12},{9,13},{1... | collective-permute-start | bytes 1376264 | tf_op jit(solution)/shard_map/ppermute | solution.py:233
  120.0 19.0 %collective-permute-start.20 = (bf16[8,14336]{1,0:T(8,128)(2,1)S(1)}, bf16[8,14336]{1,0:T(8,128)(2,1)S(1)}, u32[]{:S(2)}, u32[]{:S(2)}) collective-permute-start(bf16[8,14336]{1,0:T(8,128)(2,1)S(1)} %slice_bitcast_fusion), channel_id=1, source_target_pairs={{0,12},{1,13},{2,14},{3,15},{4,0},{5,1},{6,2},{7,3},{8,4},{9,5},{1... | collective-permute-start | bytes 688136 | tf_op jit(solution)/shard_map/ppermute | solution.py:233
  128.4 11.6 %collective-permute-start.11 = (bf16[2,8,14336]{2,1,0:T(8,128)(2,1)S(1)}, bf16[2,8,14336]{2,1,0:T(8,128)(2,1)S(1)}, u32[]{:S(2)}, u32[]{:S(2)}) collective-permute-start(bf16[2,8,14336]{2,1,0:T(8,128)(2,1)S(1)} %slice.18), channel_id=1, source_target_pairs={{0,1},{1,2},{2,3},{3,0},{4,5},{5,6},{6,7},{7,4},{8,9},{9,10},{10,1... | collective-permute-start | bytes 1376264 | tf_op jit(solution)/shard_map/ppermute | solution.py:233
  133.3 6.6 %collective-permute-start.13 = (bf16[8,14336]{1,0:T(8,128)(2,1)S(1)}, bf16[8,14336]{1,0:T(8,128)(2,1)S(1)}, u32[]{:S(2)}, u32[]{:S(2)}) collective-permute-start(bf16[8,14336]{1,0:T(8,128)(2,1)S(1)} %slice_bitcast_fusion.1), channel_id=1, source_target_pairs={{0,3},{1,0},{2,1},{3,2},{4,7},{5,4},{6,5},{7,6},{8,11},{9,8},{10,9... | collective-permute-start | bytes 688136 | tf_op jit(solution)/shard_map/ppermute | solution.py:233
